TPU v7x, 8 devices: a whole 2x2x1 slice. The times are simulated.
8 devices in a mesh: data: 8 (over z, y, x, core).
Axes of the slice: x: 2, y: 2, z: 1, core: 2. Of those that a mesh axis runs over, the one named last changes fastest.
Arguments:
- tok_ids: int32 [32768], P('data')
- grad_out: bfloat16 [32768, 256], P('data')
- n_real: int32 [8], P('data')
- embed_table: bfloat16 [30522, 256], replicated
- w_in: bfloat16 [256, 1024], replicated
- w_out: bfloat16 [1024, 256], replicated
Outputs:
- output 1: float32 [30522, 256], replicated
- output 2: float32 [256, 1024], replicated
- output 3: float32 [1024, 256], replicated
All inputs are finite; a program needn't handle non-finite values.
Results may differ from a plain program's by a relative error of at most 0.00851241.
Values are sent between devices in bfloat16 or wider.
A program may use at most 1 GiB of HBM per device.

v0:
```python
import math
import jax
import jax.numpy as jnp
from jax import lax
from jax.sharding import PartitionSpec as P

GELU_A = 0.044715
GELU_C = math.sqrt(2.0 / math.pi)


def local_grads(x_rows, grad_out, keep_mask, w_in, w_out):
    dy_kept = jnp.where(keep_mask, grad_out, jnp.zeros_like(grad_out))
    pre_act = jnp.dot(x_rows, w_in, preferred_element_type=jnp.float32).astype(jnp.bfloat16)
    z_val = pre_act.astype(jnp.float32)
    tanh_val = jnp.tanh(GELU_C * (z_val + GELU_A * z_val * z_val * z_val))
    act_bf16 = (0.5 * z_val * (1.0 + tanh_val)).astype(jnp.bfloat16)
    slope_val = 0.5 * (1.0 + tanh_val) + 0.5 * z_val * (1.0 - tanh_val * tanh_val) * GELU_C * (1.0 + 3.0 * GELU_A * z_val * z_val)
    grad_w_out = jnp.einsum('tf,td->fd', act_bf16, dy_kept, preferred_element_type=jnp.float32)
    grad_act = jnp.einsum('td,fd->tf', dy_kept, w_out, preferred_element_type=jnp.float32).astype(jnp.bfloat16)
    grad_pre = (grad_act.astype(jnp.float32) * slope_val).astype(jnp.bfloat16)
    grad_w_in = jnp.einsum('td,tf->df', x_rows, grad_pre, preferred_element_type=jnp.float32)
    grad_x = (dy_kept.astype(jnp.float32) + jnp.einsum('tf,df->td', grad_pre, w_in, preferred_element_type=jnp.float32)).astype(jnp.bfloat16)
    return grad_x, grad_w_in, grad_w_out


def solution(mesh):
    def per_device(tok_ids, grad_out, n_real, embed_table, w_in, w_out):
        keep_mask = (jnp.arange(tok_ids.shape[0]) < n_real[0])[:, None]
        x_rows = jnp.take(embed_table, tok_ids, axis=0)
        grad_x, part_in, part_out = local_grads(x_rows, grad_out, keep_mask, w_in, w_out)
        grad_w_in = lax.psum(part_in, 'data')
        grad_w_out = lax.psum(part_out, 'data')
        all_ids = lax.all_gather(tok_ids, 'data', tiled=True)
        all_rows = lax.all_gather(grad_x, 'data', tiled=True)
        grad_table = jax.ops.segment_sum(all_rows.astype(jnp.float32), all_ids, num_segments=embed_table.shape[0])
        return grad_table, grad_w_in, grad_w_out

    return jax.shard_map(per_device, mesh=mesh, in_specs=(P('data'), P('data', None), P('data'), P(), P(), P()), out_specs=(P(), P(), P()), check_vma=False)
```

profile of v0, /device:TPU:0, one launch (start us, length us, event | category | flops | bytes accessed | tf_op | source)
XLA Modules:
  0.0 327.7 jit_solution(15763934584589812157)
XLA Ops:
  7.2 0.0 copy-start
  7.2 0.0 copy-start.6
  7.2 0.0 all-gather.2.cloned.1.call-start
  7.2 0.8 compare_and_fusion
  8.0 0.7 fusion.18
  9.4 20.4 %gather_fusion = bf16[4096,256]{1,0:T(8,128)(2,1)S(1)} fusion(bf16[30522,256]{1,0:T(8,128)(2,1)} %param.9, s32[4096]{0:T(1024)S(1)} %fusion.18), kind=kCustom, calls=%fused_computation | custom fusion | bytes 4210688 | tf_op jit(solution)/shard_map/jit(_take)/gather | solution.py:29
  29.9 2.7 convolution_convert_fusion
  32.6 0.0 copy-start.4
  32.6 14.8 %fusion.8 = bf16[4096,1024]{1,0:T(8,128)(2,1)S(1)} fusion(bf16[4096,1024]{1,0:T(8,128)(2,1)S(1)} %convolution_convert_fusion, bf16[1024,256]{1,0:T(8,128)(2,1)S(1)} %copy-done.6, bf16[4096,256]{1,0:T(8,128)(2,1)} %param.7, pred[4096]{0:T(1024)(128)(4,1)S(1)} %iota_compare_fusion), kind=kOutput, calls=%fused_computation.17 | convolution fusion | flops 2240806912 | bytes 19402752 | tf_op jit(solution)/shard_map/td,fd->tf/dot_general | solution.py:19
  47.4 0.0 copy-done.1
  47.4 0.0 copy-start.7
  47.4 3.4 %copy-done.7 = bf16[4096,1024]{1,0:T(8,128)(2,1)} copy-done((bf16[4096,1024]{1,0:T(8,128)(2,1)}, bf16[4096,1024]{1,0:T(8,128)(2,1)S(1)}, u32[]{:S(2)}) %copy-start.7) | copy-done | bytes 8388632
  50.8 4.6 %fusion.16 = bf16[4096,256]{1,0:T(8,128)(2,1)} fusion(bf16[4096,1024]{1,0:T(8,128)(2,1)S(1)} %fusion.8, bf16[256,1024]{1,0:T(8,128)(2,1)S(1)} %copy-done, bf16[4096,256]{1,0:T(8,128)(2,1)S(1)} %copy-done.4, pred[4096]{0:T(1024)(128)(4,1)S(1)} %iota_compare_fusion), kind=kOutput, calls=%fused_computation.26 | convolution fusion | flops 2151677952 | bytes 13111296 | tf_op jit(solution)/shard_map/tf,df->td/dot_general | solution.py:22
  55.4 0.0 all-gather.2.cloned.1.call-update
  55.4 0.2 all-reduce.3.cloned.1.call-start
  55.7 0.0 copy-start.5
  55.7 7.0 %fusion.17 = f32[256,1024]{1,0:T(8,128)} fusion(bf16[4096,1024]{1,0:T(8,128)(2,1)} %copy-done.7, bf16[4096,256]{1,0:T(8,128)(2,1)S(1)} %gather_fusion, pred[4096]{0:T(1024)(128)(4,1)S(1)} %compare_and_fusion), kind=kOutput, calls=%fused_computation.29 | convolution fusion | flops 2148532224 | bytes 11538432 | tf_op jit(solution)/shard_map/td,tf->df/dot_general | solution.py:21
  62.7 7.4 %fusion.14 = f32[1024,256]{1,0:T(8,128)} fusion(bf16[4096,1024]{1,0:T(8,128)(2,1)S(1)} %copy-done.2, bf16[4096,256]{1,0:T(8,128)(2,1)S(1)} %copy-done.5, pred[4096]{0:T(1024)(128)(4,1)S(1)} %iota_compare_fusion), kind=kOutput, calls=%fused_computation.23 | convolution fusion | flops 2190475264 | bytes 11538432 | tf_op jit(solution)/shard_map/tf,td->fd/dot_general | solution.py:18
  70.1 0.0 all-reduce.3.cloned.1.call-update
  70.1 15.1 %all_gather.6 = s32[32768]{0:T(1024)S(1)} all-gather(s32[4096]{0:T(1024)S(1)} %copy-done.3), channel_id=1, replica_groups=mesh['data'=8] {'data'}, dimensions={0}, use_global_device_ids=true | all-gather | bytes 147456 | tf_op jit(solution)/shard_map/all_gather | solution.py:33
  85.2 58.1 %all-gather.2.cloned.1.call-done = bf16[32768,256]{1,0:T(8,128)(2,1)} async-done(((bf16[4096,256]{1,0:T(8,128)(2,1)}), bf16[32768,256]{1,0:T(8,128)(2,1)}) %all-gather.2.cloned.1.call-update) | async-done | bytes 16777232 | tf_op jit(solution)/shard_map/all_gather | solution.py:34
  143.3 173.0 %scatter_custom_fusion = f32[30522,256]{1,0:T(8,128)} fusion(s32[32768]{0:T(1024)S(1)} %all_gather.6, bf16[32768,256]{1,0:T(8,128)(2,1)} %all-gather.2.cloned.1.call-done, f32[]{:T(128)} %constant.11.clone.1), kind=kCustom, calls=%fused_computation.9 | custom fusion | flops 16777216 | bytes 48031748 | tf_op jit(solution)/shard_map/scatter-add | solution.py:35
  316.3 2.3 copy.12
  318.6 2.3 copy.13
  (11 shorter events, 0.0 us)
Async XLA Ops:
  7.2 22.7 %copy-start = (bf16[256,1024]{1,0:T(8,128)(2,1)S(1)}, bf16[256,1024]{1,0:T(8,128)(2,1)}, u32[]{:S(2)}) copy-start(bf16[256,1024]{1,0:T(8,128)(2,1)} %param.10) | copy-start | bytes 1572868
  7.2 25.4 %copy-start.6 = (bf16[1024,256]{1,0:T(8,128)(2,1)S(1)}, bf16[1024,256]{1,0:T(8,128)(2,1)}, u32[]{:S(2)}) copy-start(bf16[1024,256]{1,0:T(8,128)(2,1)} %param.11) | copy-start | bytes 1572868
  7.2 136.1 %all-gather.2.cloned.1.call-start = ((), (), s32[]{:S(2)}) async-start(), calls=%async_computation | async-start | bytes 18874368 | tf_op jit(solution)/shard_map/all_gather | solution.py:34
  32.6 14.9 %copy-start.1 = (bf16[4096,1024]{1,0:T(8,128)(2,1)}, bf16[4096,1024]{1,0:T(8,128)(2,1)S(1)}, u32[]{:S(2)}) copy-start(bf16[4096,1024]{1,0:T(8,128)(2,1)S(1)} %convolution_convert_fusion) | copy-start | bytes 25165828
  32.6 18.3 %copy-start.4 = (bf16[4096,256]{1,0:T(8,128)(2,1)S(1)}, bf16[4096,256]{1,0:T(8,128)(2,1)}, u32[]{:S(2)}) copy-start(bf16[4096,256]{1,0:T(8,128)(2,1)} %param.7) | copy-start | bytes 6291460
  47.4 3.4 %copy-start.7 = (bf16[4096,1024]{1,0:T(8,128)(2,1)}, bf16[4096,1024]{1,0:T(8,128)(2,1)S(1)}, u32[]{:S(2)}) copy-start(bf16[4096,1024]{1,0:T(8,128)(2,1)S(1)} %fusion.8) | copy-start | bytes 25165828
  55.4 260.9 %all-reduce.3.cloned.1.call-start = ((), (), s32[]{:S(2)}) async-start(), calls=%async_computation.1 | async-start | bytes 4194304 | tf_op jit(solution)/shard_map/psum | solution.py:31
  55.6 7.0 %copy-start.2 = (bf16[4096,1024]{1,0:T(8,128)(2,1)S(1)}, bf16[4096,1024]{1,0:T(8,128)(2,1)}, u32[]{:S(2)}) copy-start(bf16[4096,1024]{1,0:T(8,128)(2,1)} %copy-done.1) | copy-start | bytes 25165828
  55.7 7.0 %copy-start.5 = (bf16[4096,256]{1,0:T(8,128)(2,1)S(1)}, bf16[4096,256]{1,0:T(8,128)(2,1)}, u32[]{:S(2)}) copy-start(bf16[4096,256]{1,0:T(8,128)(2,1)} %param.7) | copy-start | bytes 6291460
  62.7 7.4 %copy-start.3 = (s32[4096]{0:T(1024)S(1)}, s32[4096]{0:T(1024)}, u32[]{:S(2)}) copy-start(s32[4096]{0:T(1024)} %param.6) | copy-start | bytes 49156
Sparse Core Ops, SparseCore 0:
  55.5 87.7 all-gather.1
  147.1 50.1 all-reduce.2
where the time goes:
time: 328 us
  other arithmetic  175 us (53%)
  waiting for transfers between devices  58.1 us (18%)
  matrix products  36.4 us (11%)
  local copies, waits for them, and re-layouts  28.4 us (9%)
  blocking collectives  15.1 us (5%)
  between operations  14.8 us (5%)
    scatter-add x1, other arithmetic, per_device(): jax.ops.segment_sum(all_rows.astype(jnp.float32), all_ids, num_segments=e...  173 us
    all_gather x1, waiting for transfers between devices, per_device(): all_rows = lax.all_gather(grad_x, 'data', tiled=True)  58.1 us
    gather x1, local copies, waits for them, and re-layouts, per_device(): x_rows = jnp.take(embed_table, tok_ids, axis=0)  20.4 us
    all_gather x1, blocking collectives, per_device(): all_ids = lax.all_gather(tok_ids, 'data', tiled=True)  15.1 us
    dot_general x1, matrix products, local_grads(): jnp.einsum('td,fd->tf', dy_kept, w_out, preferred_element_type=jnp.float32)  14.8 us
    unnamed x18, local copies, waits for them, and re-layouts  8 us
    dot_general x1, matrix products, local_grads(): jnp.einsum('tf,td->fd', act_bf16, dy_kept, preferred_element_type=jnp.flo...  7.41 us
    dot_general x1, matrix products, local_grads(): jnp.einsum('td,tf->df', x_rows, grad_pre, preferred_element_type=jnp.floa...  6.99 us
  transfers between devices with their start and end apart: 2, of which 1 were waited for; matrix products, arithmetic and copies ran while one was open for 57% of the time, Pallas kernels for 0%

commit v1 on v0

v1 whole, which is shorter than its diff:
```python
import functools
import math

import jax
import jax.numpy as jnp
from jax import lax
from jax.experimental import pallas as pl
from jax.experimental.pallas import tpu as pltpu
from jax.sharding import PartitionSpec as P

GELU_A = 0.044715
GELU_C = math.sqrt(2.0 / math.pi)

NDEV = 8
TOK = 4096
VOCAB = 30522
DIM = 256
FFN = 1024
UNIQ = 1024
HI = 128
LO = 256
STEP_TOK = 512
CHUNK_HI = 16
CHUNK = CHUNK_HI * LO
NCHUNK = -(-VOCAB // CHUNK)
LAST = VOCAB - (NCHUNK - 1) * CHUNK
BATCH = 16
META = UNIQ + HI

F32 = jnp.float32
BF16 = jnp.bfloat16
VMEM_LIMIT = 62 * 1024 * 1024


def dot(a, b, ca, cb):
    return lax.dot_general(a, b, (((ca,), (cb,)), ((), ())), preferred_element_type=F32)


def iota(shape, axis):
    return lax.broadcasted_iota(jnp.int32, shape, axis)


def dedup_kernel(n_ref, ids_ref, dy_ref, meta_ref, msum_ref):
    ids = ids_ref[...]
    ohi = (iota((HI, TOK), 0) == (ids >> 8)).astype(BF16)
    olo = (iota((LO, TOK), 0) == (ids & 255)).astype(BF16)
    present = (dot(ohi, olo, 1, 1) > 0.5).astype(BF16)
    upper = (iota((LO, LO), 0) < iota((LO, LO), 1)).astype(BF16)
    before = dot(present, upper, 1, 0)
    total = dot(present, jnp.ones((LO, UNIQ), BF16), 1, 0)
    lower = (iota((HI, HI), 1) < iota((HI, HI), 0)).astype(BF16)
    offset = dot(lower, total.astype(BF16), 1, 0)
    rank = before + offset[:, :LO]
    rank_a = jnp.floor(rank * (1.0 / 32.0))
    rank_b = (rank - 32.0 * rank_a).astype(BF16)
    rank_a = rank_a.astype(BF16)

    lane = iota((HI, UNIQ), 1).astype(F32)
    hi_of = jnp.sum(((offset + total) <= lane).astype(F32), axis=0, keepdims=True)
    hot = iota((HI, UNIQ), 0).astype(F32) == hi_of
    k_of = lane[:1] - jnp.sum(jnp.where(hot, offset, 0.0), axis=0, keepdims=True)
    upto = (before + present.astype(F32)).astype(BF16)
    row_of = dot(upto, hot.astype(BF16), 0, 0)
    lo_of = jnp.sum((row_of <= k_of).astype(F32), axis=0, keepdims=True)
    meta_ref[:, :UNIQ] = (hi_of * 256.0 + lo_of).astype(jnp.int32)
    eye = iota((HI, HI), 0) == iota((HI, HI), 1)
    meta_ref[:, UNIQ:] = jnp.sum(jnp.where(eye, offset[:, :HI], 0.0), axis=0, keepdims=True).astype(jnp.int32)

    kept = n_ref[0]
    for b in range(TOK // STEP_TOK):
        cols = slice(b * STEP_TOK, (b + 1) * STEP_TOK)
        mine = ohi[:, cols]
        pos = 32.0 * dot(rank_a, mine, 0, 0) + dot(rank_b, mine, 0, 0)
        slot = jnp.sum(pos * olo[:, cols].astype(F32), axis=0, keepdims=True)
        tok = iota((1, STEP_TOK), 1) + b * STEP_TOK
        slot = jnp.where(tok < kept, slot.astype(jnp.int32), -1)
        pick = (iota((UNIQ, STEP_TOK), 0) == slot).astype(BF16)
        part = dot(pick, dy_ref[cols, :], 1, 0)
        if b == 0:
            msum_ref[...] = part
        else:
            msum_ref[...] += part


def dedup(n_real, ids, dy):
    return pl.pallas_call(
        dedup_kernel,
        out_shape=(jax.ShapeDtypeStruct((1, META), jnp.int32), jax.ShapeDtypeStruct((UNIQ, DIM), F32)),
        in_specs=[pl.BlockSpec(memory_space=pltpu.SMEM), pl.BlockSpec(memory_space=pltpu.VMEM), pl.BlockSpec(memory_space=pltpu.VMEM)],
        out_specs=(pl.BlockSpec(memory_space=pltpu.VMEM), pl.BlockSpec(memory_space=pltpu.VMEM)),
        compiler_params=pltpu.CompilerParams(vmem_limit_bytes=VMEM_LIMIT),
        name="dedup",
    )(n_real, ids, dy)


def grads_kernel(x_ref, m_ref, w1_ref, w2_ref, dx_ref, dw1_ref, dw2_ref):
    first = pl.program_id(0) == 0
    x = x_ref[...]
    m = m_ref[...]
    m_hi = m.astype(BF16)
    m_lo = (m - m_hi.astype(F32)).astype(BF16)
    z = dot(x, w1_ref[...], 1, 0).astype(BF16).astype(F32)
    t = jnp.tanh(GELU_C * (z + GELU_A * z * z * z))
    h = (0.5 * z * (1.0 + t)).astype(BF16)
    slope = 0.5 * (1.0 + t) + 0.5 * z * (1.0 - t * t) * GELU_C * (1.0 + 3.0 * GELU_A * z * z)
    dh = (dot(m_hi, w2_ref[...], 1, 1) + dot(m_lo, w2_ref[...], 1, 1)).astype(BF16).astype(F32)
    dz = (dh * slope).astype(BF16)
    dx_ref[...] = m + dot(dz, w1_ref[...], 1, 1)
    dw1 = dot(x, dz, 0, 0)
    dw2 = dot(h, m_hi, 0, 0) + dot(h, m_lo, 0, 0)

    @pl.when(first)
    def _():
        dw1_ref[...] = dw1
        dw2_ref[...] = dw2

    @pl.when(jnp.logical_not(first))
    def _():
        dw1_ref[...] += dw1
        dw2_ref[...] += dw2


def grads(x, m, w1, w2):
    rows = 256
    return pl.pallas_call(
        grads_kernel,
        grid=(UNIQ // rows,),
        out_shape=(jax.ShapeDtypeStruct((UNIQ, DIM), F32), jax.ShapeDtypeStruct((DIM, FFN), F32), jax.ShapeDtypeStruct((FFN, DIM), F32)),
        in_specs=[pl.BlockSpec((rows, DIM), lambda i: (i, 0)), pl.BlockSpec((rows, DIM), lambda i: (i, 0)),
                  pl.BlockSpec((DIM, FFN), lambda i: (0, 0)), pl.BlockSpec((FFN, DIM), lambda i: (0, 0))],
        out_specs=(pl.BlockSpec((rows, DIM), lambda i: (i, 0)), pl.BlockSpec((DIM, FFN), lambda i: (0, 0)), pl.BlockSpec((FFN, DIM), lambda i: (0, 0))),
        compiler_params=pltpu.CompilerParams(vmem_limit_bytes=VMEM_LIMIT, dimension_semantics=("arbitrary",)),
        name="grads",
    )(x, m, w1, w2)


def table_kernel(meta_ref, rows_hbm, out_hbm, rows, acc, in_sem, out_sem):
    def in_copy(d, half):
        part = pl.ds(d * UNIQ, UNIQ)
        return pltpu.make_async_copy(rows_hbm.at[part, pl.ds(half * 128, 128)], rows.at[half, part], in_sem.at[d, half])

    for d in range(NDEV):
        for half in range(2):
            in_copy(d, half).start()

    def out_copy(c, slot, half):
        size = CHUNK if c < NCHUNK - 1 else LAST
        return pltpu.make_async_copy(acc.at[slot, half, pl.ds(0, size)], out_hbm.at[pl.ds(c * CHUNK, size), pl.ds(half * 128, 128)], out_sem.at[slot, half])

    for c in range(NCHUNK):
        slot = c % 2
        if c >= 2:
            for half in range(2):
                out_copy(c - 2, slot, half).wait()
        acc[slot, :, pl.ds(0, CHUNK)] = jnp.zeros((2, CHUNK, 128), F32)
        for d in range(NDEV):
            if c == 0:
                for half in range(2):
                    in_copy(d, half).wait()
            start = meta_ref[d, UNIQ + c * CHUNK_HI]
            end = meta_ref[d, UNIQ + (c + 1) * CHUNK_HI] if (c + 1) * CHUNK_HI < HI else UNIQ

            @pl.loop(start // BATCH, (end + BATCH - 1) // BATCH)
            def _(b):
                base = pl.multiple_of(b * BATCH, BATCH)
                at = []
                for k in range(BATCH):
                    loc = meta_ref[d, base + k] - c * CHUNK
                    at.append(jnp.where((loc >= 0) & (loc < CHUNK), loc, CHUNK))
                sums = []
                for k in range(BATCH):
                    for half in range(2):
                        sums.append(acc[slot, half, pl.ds(at[k], 1), :] + rows[half, pl.ds(d * UNIQ + base + k, 1), :])
                for k in range(BATCH):
                    for half in range(2):
                        acc[slot, half, pl.ds(at[k], 1), :] = sums[2 * k + half]
        for half in range(2):
            out_copy(c, slot, half).start()
    for c in range(max(0, NCHUNK - 2), NCHUNK):
        for half in range(2):
            out_copy(c, c % 2, half).wait()


def table(meta, rows):
    return pl.pallas_call(
        table_kernel,
        grid_spec=pltpu.PrefetchScalarGridSpec(
            num_scalar_prefetch=1, grid=(1,),
            in_specs=[pl.BlockSpec(memory_space=pl.ANY)], out_specs=pl.BlockSpec(memory_space=pl.ANY),
            scratch_shapes=[pltpu.VMEM((2, NDEV * UNIQ, 128), F32), pltpu.VMEM((2, 2, CHUNK + 8, 128), F32),
                            pltpu.SemaphoreType.DMA((NDEV, 2)), pltpu.SemaphoreType.DMA((2, 2))]),
        out_shape=jax.ShapeDtypeStruct((VOCAB, DIM), F32),
        compiler_params=pltpu.CompilerParams(vmem_limit_bytes=VMEM_LIMIT),
        name="table",
    )(meta, rows)


def solution(mesh):
    def per_device(tok_ids, grad_out, n_real, embed_table, w_in, w_out):
        meta, msum = dedup(n_real, tok_ids.reshape(1, TOK), grad_out)
        x = jnp.take(embed_table, meta[0, :UNIQ], axis=0, mode='clip')
        dx, part_in, part_out = grads(x, msum, w_in, w_out)
        grad_w_in = lax.psum(part_in, 'data')
        grad_w_out = lax.psum(part_out, 'data')
        all_meta = lax.all_gather(meta, 'data', tiled=True)
        all_rows = lax.all_gather(dx, 'data', tiled=True)
        return table(all_meta, all_rows), grad_w_in, grad_w_out

    return jax.shard_map(per_device, mesh=mesh, in_specs=(P('data'), P('data', None), P('data'), P(), P(), P()), out_specs=(P(), P(), P()), check_vma=False)
```

time: 328 us -> 158 us (0.48)
  other arithmetic: 175 us -> 0.01 us
  Pallas kernels: 0 us -> 74.1 us
  matrix products: 36.4 us -> 0 us
  waiting for transfers between devices: 58.1 us -> 36.7 us
  local copies, waits for them, and re-layouts: 28.4 us -> 17.9 us
    scatter-add x1 -> x0, other arithmetic: 173 us -> none  [per_device(): jax.ops.segment_sum(all_rows.astype(jnp.float32), all_ids, num_segments=e...]
    pallas_call x0 -> x3, Pallas kernels: none -> 74.1 us  [the longest x1 54.8 us: table(): pl.pallas_call(table_kernel, grid_spec=pltpu.PrefetchScalarGridSpec(num_s...]
    dot_general x5 -> x0, matrix products: 36.4 us -> none  [the longest x1 14.8 us: local_grads(): jnp.einsum('td,fd->tf', dy_kept, w_out, preferred_element_type=jnp.float32)]
    all_gather x1, waiting for transfers between devices: 58.1 us -> 36 us  [per_device(): all_rows = lax.all_gather(dx, 'data', tiled=True)]
    gather x1, local copies, waits for them, and re-layouts: 20.4 us -> 12.1 us  [per_device(): x = jnp.take(embed_table, meta[0, :UNIQ], axis=0, mode='clip')]
    unnamed x18 -> x3, local copies, waits for them, and re-layouts: 8 us -> 5.19 us
  transfers between devices with their start and end apart: 2 -> 2, of which waited for: 1 -> 1; matrix products, arithmetic and copies ran while one was open for 57% -> 0% of each run, Pallas kernels for 0% -> 35%
where the time goes in v1:
time: 158 us
  Pallas kernels  74.1 us (47%)
  waiting for transfers between devices  36.7 us (23%)
  local copies, waits for them, and re-layouts  17.9 us (11%)
  between operations  14.7 us (9%)
  blocking collectives  14.3 us (9%)
    pallas_call x1, Pallas kernels, table(): pl.pallas_call(table_kernel, grid_spec=pltpu.PrefetchScalarGridSpec(num_s...  54.8 us
    all_gather x1, waiting for transfers between devices, per_device(): all_rows = lax.all_gather(dx, 'data', tiled=True)  36 us
    all_gather x1, blocking collectives, per_device(): all_meta = lax.all_gather(meta, 'data', tiled=True)  14.3 us
    gather x1, local copies, waits for them, and re-layouts, per_device(): x = jnp.take(embed_table, meta[0, :UNIQ], axis=0, mode='clip')  12.1 us
    pallas_call x1, Pallas kernels, grads(): pl.pallas_call(grads_kernel, grid=(UNIQ // rows,), out_shape=(jax.ShapeDt...  10 us
    pallas_call x1, Pallas kernels, dedup(): pl.pallas_call(dedup_kernel, out_shape=(jax.ShapeDtypeStruct((1, META), j...  9.35 us
    unnamed x3, local copies, waits for them, and re-layouts  5.19 us
  transfers between devices with their start and end apart: 2, of which 1 were waited for; matrix products, arithmetic and copies ran while one was open for 0% of the time, Pallas kernels for 35%

profile of v1, /device:TPU:0, one launch (start us, length us, event | category | flops | bytes accessed | tf_op | source)
XLA Modules:
  0.0 157.9 jit_solution(9340677029583889677)
XLA Ops:
  7.2 0.0 all-gather.3.cloned.1.call-start
  7.9 9.3 %dedup.1 = (s32[1,1152]{1,0:T(1,128)}, f32[1024,256]{1,0:T(8,128)}) custom-call(s32[1]{0:T(128)S(6)} %copy.14.n_ref, s32[1,4096]{1,0:T(1,128)} %bitcast.8, bf16[4096,256]{1,0:T(8,128)(2,1)} %dy_ref.1), custom_call_target="tpu_custom_call" | custom-call | tf_op jit(solution)/shard_map/dedup/pallas_call | solution.py:86
  17.2 0.7 slice.3
  17.9 12.1 %gather_fusion = bf16[1024,256]{1,0:T(8,128)(2,1)} fusion(bf16[30522,256]{1,0:T(8,128)(2,1)} %param.9, s32[1024]{0:T(1024)S(1)} %broadcast_clamp_fusion), kind=kCustom, calls=%fused_computation | custom fusion | bytes 1052672 | tf_op jit(solution)/shard_map/jit(_take)/gather | solution.py:201
  30.0 10.0 %grads.1 = (f32[1024,256]{1,0:T(8,128)}, f32[256,1024]{1,0:T(8,128)}, f32[1024,256]{1,0:T(8,128)}) custom-call(bf16[1024,256]{1,0:T(8,128)(2,1)} %gather_fusion, f32[1024,256]{1,0:T(8,128)} %get-tuple-element.9.m_ref, bf16[256,1024]{1,0:T(8,128)(2,1)} %w1_ref.1, bf16[1024,256]{1,0:T(8,128)(2,1)} %w2_ref.1), custom_call_target="tpu_custom_call" | custom-call | tf_op jit(solution)/shard_map/grads/pallas_call | solution.py:125
  40.0 0.0 all-gather.3.cloned.1.call-update
  40.0 0.0 all-reduce.3.cloned.1.call-start
  40.1 0.7 all-reduce.3.cloned.1.call-update
  40.8 14.3 %all-gather = s32[8,1,1152]{2,1,0:T(1,128)S(1)} all-gather(s32[1,1,1152]{2,1,0:T(1,128)} %bitcast.7), channel_id=1, replica_groups=mesh['data'=8] {'data'}, dimensions={0}, use_global_device_ids=true | all-gather | bytes 41472 | tf_op jit(solution)/shard_map/all_gather | solution.py:205
  55.1 0.6 copy.11
  55.7 36.0 %all-gather.3.cloned.1.call-done.rows_hbm = f32[8192,256]{1,0:T(8,128)} async-done(((f32[1024,256]{1,0:T(8,128)}), f32[8192,256]{1,0:T(8,128)}) %all-gather.3.cloned.1.call-update) | async-done | bytes 8388624 | tf_op jit(solution)/shard_map/all_gather | solution.py:206
  91.7 54.8 %table.1 = f32[30522,256]{1,0:T(8,128)} custom-call(s32[8,1152]{1,0:T(8,128)} %bitcast.6, f32[8192,256]{1,0:T(8,128)} %all-gather.3.cloned.1.call-done.rows_hbm), custom_call_target="tpu_custom_call" | custom-call | tf_op jit(solution)/shard_map/table/pallas_call | solution.py:185
  146.5 0.0 all-reduce.3.cloned.1.call-done
  146.5 2.3 %copy.15 = f32[256,1024]{1,0:T(8,128)} copy(f32[256,1024]{1,0:T(8,128)} %get-tuple-element.16) | data formatting | bytes 2097152
  148.8 2.3 %copy.16 = f32[1024,256]{1,0:T(8,128)} copy(f32[1024,256]{1,0:T(8,128)} %get-tuple-element.17) | data formatting | bytes 2097152
  (1 shorter events, 0.0 us)
Async XLA Ops:
  7.2 84.5 %all-gather.3.cloned.1.call-start = ((), (), s32[]{:S(2)}) async-start(), calls=%async_computation | async-start | bytes 9437184 | tf_op jit(solution)/shard_map/all_gather | solution.py:206
  40.0 106.5 %all-reduce.3.cloned.1.call-start = ((), (), s32[]{:S(2)}) async-start(), calls=%async_computation.1 | async-start | bytes 4194304 | tf_op jit(solution)/shard_map/psum | solution.py:203
Sparse Core Ops, SparseCore 0:
  40.1 51.5 all-gather.2
  94.9 50.1 all-reduce.2

commit v2 on v1

--- a/solution.py
+++ b/solution.py
@@ -24,7 +24,9 @@
 CHUNK = CHUNK_HI * LO
 NCHUNK = -(-VOCAB // CHUNK)
 LAST = VOCAB - (NCHUNK - 1) * CHUNK
-BATCH = 16
+BATCH = 8
+PADDED = 30528
+ZERO = 192
 META = UNIQ + HI
 
 F32 = jnp.float32
@@ -134,65 +136,77 @@
     )(x, m, w1, w2)
 
 
-def table_kernel(meta_ref, rows_hbm, out_hbm, rows, acc, in_sem, out_sem):
+def table_kernel(uid_ref, off_ref, rows_hbm, out_hbm, rows, acc, in_sem, out_sem):
     def in_copy(d, half):
         part = pl.ds(d * UNIQ, UNIQ)
         return pltpu.make_async_copy(rows_hbm.at[part, pl.ds(half * 128, 128)], rows.at[half, part], in_sem.at[d, half])
 
+    def out_copy(c, half):
+        part = pl.ds(c * CHUNK, CHUNK if c < NCHUNK - 1 else LAST)
+        return pltpu.make_async_copy(acc.at[half, part], out_hbm.at[part, pl.ds(half * 128, 128)], out_sem.at[c, half])
+
     for d in range(NDEV):
         for half in range(2):
             in_copy(d, half).start()
 
-    def out_copy(c, slot, half):
-        size = CHUNK if c < NCHUNK - 1 else LAST
-        return pltpu.make_async_copy(acc.at[slot, half, pl.ds(0, size)], out_hbm.at[pl.ds(c * CHUNK, size), pl.ds(half * 128, 128)], out_sem.at[slot, half])
+    @pl.loop(0, PADDED // ZERO)
+    def _(i):
+        part = pl.ds(pl.multiple_of(i * ZERO, ZERO), ZERO)
+        for half in range(2):
+            acc[half, part] = jnp.zeros((ZERO, 128), F32)
+
+    for d in range(NDEV):
+        for half in range(2):
+            in_copy(d, half).wait()
 
     for c in range(NCHUNK):
-        slot = c % 2
-        if c >= 2:
-            for half in range(2):
-                out_copy(c - 2, slot, half).wait()
-        acc[slot, :, pl.ds(0, CHUNK)] = jnp.zeros((2, CHUNK, 128), F32)
         for d in range(NDEV):
-            if c == 0:
+            first = (off_ref[d * HI + c * CHUNK_HI] + BATCH - 1) // BATCH
+            last = (off_ref[d * HI + (c + 1) * CHUNK_HI] + BATCH - 1) // BATCH if c < NCHUNK - 1 else UNIQ // BATCH
+
+            def fetch(b):
+                base = pl.multiple_of(d * UNIQ + b * BATCH, BATCH)
+                sums = []
                 for half in range(2):
-                    in_copy(d, half).wait()
-            start = meta_ref[d, UNIQ + c * CHUNK_HI]
-            end = meta_ref[d, UNIQ + (c + 1) * CHUNK_HI] if (c + 1) * CHUNK_HI < HI else UNIQ
-
-            @pl.loop(start // BATCH, (end + BATCH - 1) // BATCH)
-            def _(b):
-                base = pl.multiple_of(b * BATCH, BATCH)
-                at = []
-                for k in range(BATCH):
-                    loc = meta_ref[d, base + k] - c * CHUNK
-                    at.append(jnp.where((loc >= 0) & (loc < CHUNK), loc, CHUNK))
-                sums = []
-                for k in range(BATCH):
-                    for half in range(2):
-                        sums.append(acc[slot, half, pl.ds(at[k], 1), :] + rows[half, pl.ds(d * UNIQ + base + k, 1), :])
-                for k in range(BATCH):
-                    for half in range(2):
-                        acc[slot, half, pl.ds(at[k], 1), :] = sums[2 * k + half]
-        for half in range(2):
-            out_copy(c, slot, half).start()
-    for c in range(max(0, NCHUNK - 2), NCHUNK):
-        for half in range(2):
-            out_copy(c, c % 2, half).wait()
+                    for k in range(BATCH):
+                        sums.append(acc[half, pl.ds(uid_ref[base + k], 1), :] + rows[half, pl.ds(base + k, 1), :])
+                return sums
+
+            def put(b, sums):
+                base = pl.multiple_of(d * UNIQ + b * BATCH, BATCH)
+                for half in range(2):
+                    for k in range(BATCH):
+                        acc[half, pl.ds(uid_ref[base + k], 1), :] = sums[half * BATCH + k]
+
+            def step(b, sums):
+                ahead = fetch(b)
+                put(b - 1, sums)
+                return ahead
+
+            @pl.when(last > first)
+            def _():
+                sums = lax.fori_loop(first + 1, last, step, fetch(first))
+                put(last - 1, sums)
+
+        for half in range(2):
+            out_copy(c, half).start()
+    for c in range(NCHUNK):
+        for half in range(2):
+            out_copy(c, half).wait()
 
 
 def table(meta, rows):
     return pl.pallas_call(
         table_kernel,
         grid_spec=pltpu.PrefetchScalarGridSpec(
-            num_scalar_prefetch=1, grid=(1,),
+            num_scalar_prefetch=2, grid=(1,),
             in_specs=[pl.BlockSpec(memory_space=pl.ANY)], out_specs=pl.BlockSpec(memory_space=pl.ANY),
-            scratch_shapes=[pltpu.VMEM((2, NDEV * UNIQ, 128), F32), pltpu.VMEM((2, 2, CHUNK + 8, 128), F32),
-                            pltpu.SemaphoreType.DMA((NDEV, 2)), pltpu.SemaphoreType.DMA((2, 2))]),
+            scratch_shapes=[pltpu.VMEM((2, NDEV * UNIQ, 128), F32), pltpu.VMEM((2, PADDED, 128), F32),
+                            pltpu.SemaphoreType.DMA((NDEV, 2)), pltpu.SemaphoreType.DMA((NCHUNK, 2))]),
         out_shape=jax.ShapeDtypeStruct((VOCAB, DIM), F32),
         compiler_params=pltpu.CompilerParams(vmem_limit_bytes=VMEM_LIMIT),
         name="table",
-    )(meta, rows)
+    )(meta[:, :UNIQ].reshape(-1), meta[:, UNIQ:].reshape(-1), rows)
 
 
 def solution(mesh):

time: 158 us -> 157 us (level)
  Pallas kernels: 74.1 us -> 50.3 us
  waiting for transfers between devices: 36.7 us -> 58.5 us
    pallas_call x1, Pallas kernels: 54.8 us -> 31 us  [table(): pl.pallas_call(table_kernel, grid_spec=pltpu.PrefetchScalarGridSpec(num_s...]
    psum x1, waiting for transfers between devices: 0.02 us -> 22.4 us  [per_device(): grad_w_in = lax.psum(part_in, 'data')]
    unnamed x3 -> x5, local copies, waits for them, and re-layouts: 5.19 us -> 5.2 us
  transfers between devices with their start and end apart: 2 -> 2, of which waited for: 1 -> 2; matrix products, arithmetic and copies ran while one was open for 0% -> 1% of each run, Pallas kernels for 35% -> 20%
where the time goes in v2:
time: 157 us
  waiting for transfers between devices  58.5 us (37%)
  Pallas kernels  50.3 us (32%)
  local copies, waits for them, and re-layouts  18.5 us (12%)
  between operations  14.7 us (9%)
  blocking collectives  14.3 us (9%)
    all_gather x1, waiting for transfers between devices, per_device(): all_rows = lax.all_gather(dx, 'data', tiled=True)  35.4 us
    pallas_call x1, Pallas kernels, table(): pl.pallas_call(table_kernel, grid_spec=pltpu.PrefetchScalarGridSpec(num_s...  31 us
    psum x1, waiting for transfers between devices, per_device(): grad_w_in = lax.psum(part_in, 'data')  22.4 us
    all_gather x1, blocking collectives, per_device(): all_meta = lax.all_gather(meta, 'data', tiled=True)  14.3 us
    gather x1, local copies, waits for them, and re-layouts, per_device(): x = jnp.take(embed_table, meta[0, :UNIQ], axis=0, mode='clip')  12.1 us
    pallas_call x1, Pallas kernels, grads(): pl.pallas_call(grads_kernel, grid=(UNIQ // rows,), out_shape=(jax.ShapeDt...  10 us
    pallas_call x1, Pallas kernels, dedup(): pl.pallas_call(dedup_kernel, out_shape=(jax.ShapeDtypeStruct((1, META), j...  9.35 us
    unnamed x5, local copies, waits for them, and re-layouts  5.2 us
  transfers between devices with their start and end apart: 2, of which 2 were waited for; matrix products, arithmetic and copies ran while one was open for 1% of the time, Pallas kernels for 20%

profile of v2, /device:TPU:0, one launch (start us, length us, event | category | flops | bytes accessed | tf_op | source)
XLA Modules:
  0.0 156.5 jit_solution(16700554292065713378)
XLA Ops:
  7.2 0.0 all-gather.3.cloned.1.call-start
  7.9 9.3 %dedup.1 = (s32[1,1152]{1,0:T(1,128)}, f32[1024,256]{1,0:T(8,128)}) custom-call(s32[1]{0:T(128)S(6)} %copy.17.n_ref, s32[1,4096]{1,0:T(1,128)} %bitcast.17, bf16[4096,256]{1,0:T(8,128)(2,1)} %dy_ref.1), custom_call_target="tpu_custom_call" | custom-call | tf_op jit(solution)/shard_map/dedup/pallas_call | solution.py:88
  17.2 0.7 slice.11
  17.9 12.1 %gather_fusion = bf16[1024,256]{1,0:T(8,128)(2,1)} fusion(bf16[30522,256]{1,0:T(8,128)(2,1)} %param.9, s32[1024]{0:T(1024)S(1)} %broadcast_clamp_fusion), kind=kCustom, calls=%fused_computation | custom fusion | bytes 1052672 | tf_op jit(solution)/shard_map/jit(_take)/gather | solution.py:215
  30.0 10.0 %grads.1 = (f32[1024,256]{1,0:T(8,128)}, f32[256,1024]{1,0:T(8,128)}, f32[1024,256]{1,0:T(8,128)}) custom-call(bf16[1024,256]{1,0:T(8,128)(2,1)} %gather_fusion, f32[1024,256]{1,0:T(8,128)} %get-tuple-element.9.m_ref, bf16[256,1024]{1,0:T(8,128)(2,1)} %w1_ref.1, bf16[1024,256]{1,0:T(8,128)(2,1)} %w2_ref.1), custom_call_target="tpu_custom_call" | custom-call | tf_op jit(solution)/shard_map/grads/pallas_call | solution.py:127
  40.0 0.0 all-gather.3.cloned.1.call-update
  40.0 0.0 all-reduce.3.cloned.1.call-start
  40.1 0.7 all-reduce.3.cloned.1.call-update
  40.8 14.3 %all-gather = s32[8,1,1152]{2,1,0:T(1,128)S(1)} all-gather(s32[1,1,1152]{2,1,0:T(1,128)} %bitcast.16), channel_id=1, replica_groups=mesh['data'=8] {'data'}, dimensions={0}, use_global_device_ids=true | all-gather | bytes 41472 | tf_op jit(solution)/shard_map/all_gather | solution.py:219
  55.1 0.6 copy.14
  55.7 0.6 slice_bitcast_fusion.1.off_ref
  56.3 35.4 %all-gather.3.cloned.1.call-done.rows_hbm = f32[8192,256]{1,0:T(8,128)} async-done(((f32[1024,256]{1,0:T(8,128)}), f32[8192,256]{1,0:T(8,128)}) %all-gather.3.cloned.1.call-update) | async-done | bytes 8388624 | tf_op jit(solution)/shard_map/all_gather | solution.py:220
  91.7 31.0 %table.1 = f32[30522,256]{1,0:T(8,128)} custom-call(s32[8192]{0:T(1024)} %bitcast.15, s32[1024]{0:T(1024)} %slice_bitcast_fusion.1.off_ref, f32[8192,256]{1,0:T(8,128)} %all-gather.3.cloned.1.call-done.rows_hbm), custom_call_target="tpu_custom_call" | custom-call | tf_op jit(solution)/shard_map/table/pallas_call | solution.py:199
  122.7 22.4 %all-reduce.3.cloned.1.call-done = (f32[256,1024]{1,0:T(8,128)}, f32[1024,256]{1,0:T(8,128)}) async-done(((f32[256,1024]{1,0:T(8,128)}, f32[1024,256]{1,0:T(8,128)}), (f32[256,1024]{1,0:T(8,128)}, f32[1024,256]{1,0:T(8,128)})) %all-reduce.3.cloned.1.call-update) | async-done | bytes 2097168 | tf_op jit(solution)/shard_map/psum | solution.py:217
  145.1 2.3 %copy.18 = f32[256,1024]{1,0:T(8,128)} copy(f32[256,1024]{1,0:T(8,128)} %get-tuple-element.16) | data formatting | bytes 2097152
  147.4 2.3 %copy.19 = f32[1024,256]{1,0:T(8,128)} copy(f32[1024,256]{1,0:T(8,128)} %get-tuple-element.17) | data formatting | bytes 2097152
  (3 shorter events, 0.0 us)
Async XLA Ops:
  7.2 84.5 %all-gather.3.cloned.1.call-start = ((), (), s32[]{:S(2)}) async-start(), calls=%async_computation | async-start | bytes 9437184 | tf_op jit(solution)/shard_map/all_gather | solution.py:220
  40.0 105.1 %all-reduce.3.cloned.1.call-start = ((), (), s32[]{:S(2)}) async-start(), calls=%async_computation.1 | async-start | bytes 4194304 | tf_op jit(solution)/shard_map/psum | solution.py:217
Sparse Core Ops, SparseCore 0:
  40.1 51.5 all-gather.2
  94.9 50.1 all-reduce.2

commit v3 on v2

--- a/solution.py
+++ b/solution.py
@@ -27,6 +27,9 @@
 BATCH = 8
 PADDED = 30528
 ZERO = 192
+PIECES = 4
+PIECE = UNIQ // PIECES
+QROWS = DIM // 4
 META = UNIQ + HI
 
 F32 = jnp.float32
@@ -95,45 +98,152 @@
     )(n_real, ids, dy)
 
 
-def grads_kernel(x_ref, m_ref, w1_ref, w2_ref, dx_ref, dw1_ref, dw2_ref):
-    first = pl.program_id(0) == 0
-    x = x_ref[...]
-    m = m_ref[...]
-    m_hi = m.astype(BF16)
-    m_lo = (m - m_hi.astype(F32)).astype(BF16)
-    z = dot(x, w1_ref[...], 1, 0).astype(BF16).astype(F32)
-    t = jnp.tanh(GELU_C * (z + GELU_A * z * z * z))
-    h = (0.5 * z * (1.0 + t)).astype(BF16)
-    slope = 0.5 * (1.0 + t) + 0.5 * z * (1.0 - t * t) * GELU_C * (1.0 + 3.0 * GELU_A * z * z)
-    dh = (dot(m_hi, w2_ref[...], 1, 1) + dot(m_lo, w2_ref[...], 1, 1)).astype(BF16).astype(F32)
-    dz = (dh * slope).astype(BF16)
-    dx_ref[...] = m + dot(dz, w1_ref[...], 1, 1)
-    dw1 = dot(x, dz, 0, 0)
-    dw2 = dot(h, m_hi, 0, 0) + dot(h, m_lo, 0, 0)
-
-    @pl.when(first)
-    def _():
-        dw1_ref[...] = dw1
-        dw2_ref[...] = dw2
-
-    @pl.when(jnp.logical_not(first))
-    def _():
-        dw1_ref[...] += dw1
-        dw2_ref[...] += dw2
-
-
-def grads(x, m, w1, w2):
-    rows = 256
+def exchange_kernel(x_ref, m_ref, w1_ref, w2_ref, meta_ref, rows_ref, meta_out, red_ref,
+                    dx, part, pin, chip, rs, fin, row_send, row_recv, meta_send, meta_recv, w_send, w_recv, own_sem):
+    me = lax.axis_index('data')
+    core, px, py = me % 2, (me // 2) % 2, me // 4
+
+    def dev(r):
+        return me + (r & 1) * (1 - 2 * core) + ((r >> 1) & 1) * (2 - 4 * px) + ((r >> 2) & 1) * (4 - 8 * py)
+
+    def remote(src, dst, send, recv, r):
+        return pltpu.make_async_remote_copy(src_ref=src, dst_ref=dst, send_sem=send, recv_sem=recv, device_id=(dev(r),), device_id_type=pl.DeviceIdType.MESH)
+
+    barrier = pltpu.get_barrier_semaphore()
+    for r in (1, 2, 4, 6):
+        pl.semaphore_signal(barrier, inc=1, device_id=(dev(r),), device_id_type=pl.DeviceIdType.MESH)
+    pl.semaphore_wait(barrier, 4)
+
+    sent = []
+
+    def rows_at(r, k):
+        return rows_ref.at[pl.ds(pl.multiple_of(dev(r) * UNIQ + k * PIECE, PIECE), PIECE)]
+
+    def send_rows(block, k, to, src=None):
+        copy = remote(rows_at(block, k) if src is None else src, rows_at(block, k), row_send.at[block, k, to // 2], row_recv.at[block ^ to, k], to)
+        copy.start()
+        sent.append(copy)
+
+    def got_rows(block, k):
+        remote(rows_at(block, k), rows_at(block, k), row_send.at[block, k, 0], row_recv.at[block, k], 1).wait_recv()
+
+    def send_meta(block, to):
+        src = meta_ref if block == 0 else meta_out.at[dev(block)]
+        copy = remote(src, meta_out.at[dev(block)], meta_send.at[block, to // 2], meta_recv.at[block ^ to], to)
+        copy.start()
+        sent.append(copy)
+
+    def got_meta(block):
+        at = meta_out.at[dev(block)]
+        remote(at, at, meta_send.at[block, 0], meta_recv.at[block], 1).wait_recv()
+
+    own = [pltpu.make_async_copy(meta_ref, meta_out.at[me], own_sem.at[PIECES])]
+    own[0].start()
+    for to in (1, 2, 4, 6):
+        send_meta(0, to)
+
+    for k in range(PIECES):
+        part_rows = pl.ds(k * PIECE, PIECE)
+        x = x_ref[part_rows, :]
+        m = m_ref[part_rows, :]
+        m_hi = m.astype(BF16)
+        m_lo = (m - m_hi.astype(F32)).astype(BF16)
+        z = dot(x, w1_ref[...], 1, 0).astype(BF16).astype(F32)
+        t = jnp.tanh(GELU_C * (z + GELU_A * z * z * z))
+        h = (0.5 * z * (1.0 + t)).astype(BF16)
+        slope = 0.5 * (1.0 + t) + 0.5 * z * (1.0 - t * t) * GELU_C * (1.0 + 3.0 * GELU_A * z * z)
+        dh = (dot(m_hi, w2_ref[...], 1, 1) + dot(m_lo, w2_ref[...], 1, 1)).astype(BF16).astype(F32)
+        dz = (dh * slope).astype(BF16)
+        dx[part_rows, :] = m + dot(dz, w1_ref[...], 1, 1)
+        dw1 = dot(x, dz, 0, 0)
+        dw2 = dot(m_hi, h, 0, 0) + dot(m_lo, h, 0, 0)
+        part[0] = dw1 if k == 0 else part[0] + dw1
+        part[1] = dw2 if k == 0 else part[1] + dw2
+        src = dx.at[part_rows]
+        for to in (2, 4, 1):
+            send_rows(0, k, to, src)
+        copy = pltpu.make_async_copy(src, rows_at(0, k), own_sem.at[k])
+        copy.start()
+        own.append(copy)
+
+    def w_copy(src, dst, i, to):
+        copy = remote(src, dst, w_send.at[i], w_recv.at[i], to)
+        copy.start()
+        sent.append(copy)
+
+    def quarter(r):
+        return pl.ds(pl.multiple_of((dev(r) // 2) * QROWS, QROWS), QROWS)
+
+    w_copy(part.at[1 - core], pin, 0, 1)
+    remote(pin, pin, w_send.at[0], w_recv.at[0], 1).wait_recv()
+    chip[...] = part[core] + pin[...]
+    for i, to in enumerate((2, 4, 6)):
+        w_copy(chip.at[quarter(to)], rs.at[i], 1 + i, to)
+
+    for block in (2, 4, 6):
+        got_meta(block)
+        send_meta(block, 1)
+
+    for k in range(PIECES):
+        got_rows(2, k)
+        if k < PIECES // 2:
+            send_rows(2, k, 4)
+        send_rows(2, k, 1)
+        got_rows(4, k)
+        if k >= PIECES // 2:
+            send_rows(4, k, 2)
+        send_rows(4, k, 1)
+
+    for i, to in enumerate((2, 4, 6)):
+        remote(rs.at[i], rs.at[i], w_send.at[1 + i], w_recv.at[1 + i], to).wait_recv()
+    fin[...] = (chip[quarter(0), :] + rs[0]) + (rs[1] + rs[2])
+
+    def red_at(r):
+        return red_ref.at[(core + r) % 2, quarter(r)]
+
+    for i, to in enumerate((2, 4, 6)):
+        w_copy(fin, red_at(0), 4 + i, to)
+    w_copy(fin, red_at(0), 7, 1)
+    copy = pltpu.make_async_copy(fin, red_at(0), own_sem.at[PIECES + 1])
+    copy.start()
+    own.append(copy)
+
+    for k in range(PIECES):
+        got_rows(6, k)
+        send_rows(6, k, 1)
+
+    for i, block in enumerate((2, 4, 6)):
+        remote(red_at(block), red_at(block), w_send.at[4 + i], w_recv.at[4 + i], 1).wait_recv()
+        w_copy(red_at(block), red_at(block), 8 + i, 1)
+
+    for block in (1, 3, 5, 7):
+        got_meta(block)
+        for k in range(PIECES):
+            got_rows(block, k)
+    for i, block in enumerate((1, 3, 5, 7)):
+        remote(red_at(block), red_at(block), w_send.at[7 + i], w_recv.at[7 + i], 1).wait_recv()
+    for copy in sent:
+        copy.wait_send()
+    for copy in own:
+        copy.wait()
+
+
+def exchange(x, m, w1, w2, meta):
+    vmem = pl.BlockSpec(memory_space=pltpu.VMEM)
+    hbm = pl.BlockSpec(memory_space=pl.ANY)
     return pl.pallas_call(
-        grads_kernel,
-        grid=(UNIQ // rows,),
-        out_shape=(jax.ShapeDtypeStruct((UNIQ, DIM), F32), jax.ShapeDtypeStruct((DIM, FFN), F32), jax.ShapeDtypeStruct((FFN, DIM), F32)),
-        in_specs=[pl.BlockSpec((rows, DIM), lambda i: (i, 0)), pl.BlockSpec((rows, DIM), lambda i: (i, 0)),
-                  pl.BlockSpec((DIM, FFN), lambda i: (0, 0)), pl.BlockSpec((FFN, DIM), lambda i: (0, 0))],
-        out_specs=(pl.BlockSpec((rows, DIM), lambda i: (i, 0)), pl.BlockSpec((DIM, FFN), lambda i: (0, 0)), pl.BlockSpec((FFN, DIM), lambda i: (0, 0))),
-        compiler_params=pltpu.CompilerParams(vmem_limit_bytes=VMEM_LIMIT, dimension_semantics=("arbitrary",)),
-        name="grads",
-    )(x, m, w1, w2)
+        exchange_kernel,
+        out_shape=(jax.ShapeDtypeStruct((NDEV * UNIQ, DIM), F32), jax.ShapeDtypeStruct((NDEV, 1, META), jnp.int32), jax.ShapeDtypeStruct((2, DIM, FFN), F32)),
+        in_specs=[vmem] * 5,
+        out_specs=(hbm, vmem, hbm),
+        scratch_shapes=[
+            pltpu.VMEM((UNIQ, DIM), F32), pltpu.VMEM((2, DIM, FFN), F32), pltpu.VMEM((DIM, FFN), F32), pltpu.VMEM((DIM, FFN), F32),
+            pltpu.VMEM((3, QROWS, FFN), F32), pltpu.VMEM((QROWS, FFN), F32),
+            pltpu.SemaphoreType.DMA((8, PIECES, 4)), pltpu.SemaphoreType.DMA((8, PIECES)), pltpu.SemaphoreType.DMA((8, 4)), pltpu.SemaphoreType.DMA((8,)),
+            pltpu.SemaphoreType.DMA((11,)), pltpu.SemaphoreType.DMA((11,)), pltpu.SemaphoreType.DMA((PIECES + 2,))],
+        compiler_params=pltpu.CompilerParams(vmem_limit_bytes=VMEM_LIMIT, collective_id=0, has_side_effects=True),
+        name="exchange",
+    )(x, m, w1, w2, meta)
 
 
 def table_kernel(uid_ref, off_ref, rows_hbm, out_hbm, rows, acc, in_sem, out_sem):
@@ -213,11 +323,7 @@
     def per_device(tok_ids, grad_out, n_real, embed_table, w_in, w_out):
         meta, msum = dedup(n_real, tok_ids.reshape(1, TOK), grad_out)
         x = jnp.take(embed_table, meta[0, :UNIQ], axis=0, mode='clip')
-        dx, part_in, part_out = grads(x, msum, w_in, w_out)
-        grad_w_in = lax.psum(part_in, 'data')
-        grad_w_out = lax.psum(part_out, 'data')
-        all_meta = lax.all_gather(meta, 'data', tiled=True)
-        all_rows = lax.all_gather(dx, 'data', tiled=True)
-        return table(all_meta, all_rows), grad_w_in, grad_w_out
+        all_rows, all_meta, red = exchange(x, msum, w_in, w_out, meta)
+        return table(all_meta[:, 0], all_rows), red[0], red[1].T
 
     return jax.shard_map(per_device, mesh=mesh, in_specs=(P('data'), P('data', None), P('data'), P(), P(), P()), out_specs=(P(), P(), P()), check_vma=False)

time: 157 us -> 130 us (0.83)
  Pallas kernels: 50.3 us -> 109 us
  waiting for transfers between devices: 58.5 us -> 0 us
  blocking collectives: 14.3 us -> 0 us
  between operations: 14.7 us -> 1.45 us
    pallas_call x1, Pallas kernels: 10 us -> 69.1 us  [exchange(): pl.pallas_call(exchange_kernel, out_shape=(jax.ShapeDtypeStruct((NDEV * U...]
    all_gather x1 -> x0, waiting for transfers between devices: 35.4 us -> none  [per_device(): all_rows = lax.all_gather(dx, 'data', tiled=True)]
    psum x1 -> x0, waiting for transfers between devices: 22.4 us -> none  [per_device(): grad_w_in = lax.psum(part_in, 'data')]
    all_gather x1 -> x0, blocking collectives: 14.3 us -> none  [per_device(): all_meta = lax.all_gather(meta, 'data', tiled=True)]
    transpose x0 -> x1, local copies, waits for them, and re-layouts: none -> 2.7 us  [per_device(): return (table(all_meta[:, 0], all_rows), red[0], red[1].T)]
    unnamed x5 -> x4, local copies, waits for them, and re-layouts: 5.2 us -> 2.71 us
  transfers between devices with their start and end apart: 2 -> 0, of which waited for: 2 -> 0; matrix products, arithmetic and copies ran while one was open for 1% -> 0% of each run, Pallas kernels for 20% -> 0%
where the time goes in v3:
time: 130 us
  Pallas kernels  109 us (84%)
  local copies, waits for them, and re-layouts  18.9 us (15%)
  between operations  1.45 us (1%)
    pallas_call x1, Pallas kernels, exchange(): pl.pallas_call(exchange_kernel, out_shape=(jax.ShapeDtypeStruct((NDEV * U...  69.1 us
    pallas_call x1, Pallas kernels, table(): pl.pallas_call(table_kernel, grid_spec=pltpu.PrefetchScalarGridSpec(num_s...  30.9 us
    gather x1, local copies, waits for them, and re-layouts, per_device(): x = jnp.take(embed_table, meta[0, :UNIQ], axis=0, mode='clip')  12.2 us
    pallas_call x1, Pallas kernels, dedup(): pl.pallas_call(dedup_kernel, out_shape=(jax.ShapeDtypeStruct((1, META), j...  9.35 us
    unnamed x4, local copies, waits for them, and re-layouts  2.71 us
    transpose x1, local copies, waits for them, and re-layouts, per_device(): return (table(all_meta[:, 0], all_rows), red[0], red[1].T)  2.7 us

profile of v3, /device:TPU:0, one launch (start us, length us, event | category | flops | bytes accessed | tf_op | source)
XLA Modules:
  0.0 129.7 jit_solution(5751065199007489800)
XLA Ops:
  1.3 9.3 %dedup.1 = (s32[1,1152]{1,0:T(1,128)}, f32[1024,256]{1,0:T(8,128)}) custom-call(s32[1]{0:T(128)S(6)} %copy.16.n_ref, s32[1,4096]{1,0:T(1,128)} %bitcast.21, bf16[4096,256]{1,0:T(8,128)(2,1)} %dy_ref.1), custom_call_target="tpu_custom_call" | custom-call | tf_op jit(solution)/shard_map/dedup/pallas_call | solution.py:91
  10.6 0.7 slice.15
  11.3 12.2 %gather_fusion = bf16[1024,256]{1,0:T(8,128)(2,1)} fusion(bf16[30522,256]{1,0:T(8,128)(2,1)} %param.9, s32[1024]{0:T(1024)S(1)} %broadcast_clamp_fusion), kind=kCustom, calls=%fused_computation | custom fusion | bytes 1052672 | tf_op jit(solution)/shard_map/jit(_take)/gather | solution.py:325
  23.6 69.1 %exchange.1 = (f32[8192,256]{1,0:T(8,128)}, s32[8,1,1152]{2,1,0:T(1,128)}, f32[2,256,1024]{2,1,0:T(8,128)}) custom-call(bf16[1024,256]{1,0:T(8,128)(2,1)} %gather_fusion, f32[1024,256]{1,0:T(8,128)} %get-tuple-element.9.m_ref, bf16[256,1024]{1,0:T(8,128)(2,1)} %w1_ref.1, bf16[1024,256]{1,0:T(8,128)(2,1)} %w2_ref.1, s32[1,1152]{1,0:T(1,128)} %get-tuple-element.8.meta_ref), custom_call_target="tpu_custom_call" | custom-call | tf_op jit(solution)/shard_map/exchange/pallas_call | solution.py:234
  92.6 0.8 copy.14
  93.4 0.6 slice_bitcast_fusion.3.off_ref
  94.0 0.6 copy.15
  94.6 2.7 %slice_bitcast_fusion = (f32[1024,256]{0,1:T(8,128)S(1)}, f32[256,1024]{1,0:T(8,128)}) fusion(f32[2,256,1024]{2,1,0:T(8,128)} %get-tuple-element.12), kind=kLoop, calls=%fused_computation.1 | loop fusion | bytes 4194304 | tf_op jit(solution)/shard_map/transpose | solution.py:327
  97.3 1.3 %copy.9 = f32[1024,256]{1,0:T(8,128)} copy(f32[1024,256]{0,1:T(8,128)S(1)} %get-tuple-element.16) | data formatting | bytes 2097152
  98.6 30.9 %table.1 = f32[30522,256]{1,0:T(8,128)} custom-call(s32[8192]{0:T(1024)} %bitcast.20, s32[1024]{0:T(1024)} %slice_bitcast_fusion.3.off_ref, f32[8192,256]{1,0:T(8,128)} %get-tuple-element.11.rows_hbm), custom_call_target="tpu_custom_call" | custom-call | tf_op jit(solution)/shard_map/table/pallas_call | solution.py:309
  (2 shorter events, 0.0 us)

commit v4 on v3

--- a/solution.py
+++ b/solution.py
@@ -29,7 +29,7 @@
 ZERO = 192
 PIECES = 4
 PIECE = UNIQ // PIECES
-QROWS = DIM // 4
+QROWS = FFN // 4
 META = UNIQ + HI
 
 F32 = jnp.float32
@@ -155,9 +155,11 @@
         dh = (dot(m_hi, w2_ref[...], 1, 1) + dot(m_lo, w2_ref[...], 1, 1)).astype(BF16).astype(F32)
         dz = (dh * slope).astype(BF16)
         dx[part_rows, :] = m + dot(dz, w1_ref[...], 1, 1)
-        dw1 = dot(x, dz, 0, 0)
-        dw2 = dot(m_hi, h, 0, 0) + dot(m_lo, h, 0, 0)
-        part[0] = dw1 if k == 0 else part[0] + dw1
+        for q in range(FFN // DIM):
+            cols = slice(q * DIM, (q + 1) * DIM)
+            dw1 = dot(x, dz[:, cols], 0, 0)
+            part[0, cols] = dw1 if k == 0 else part[0, cols] + dw1
+        dw2 = dot(h, m_hi, 0, 0) + dot(h, m_lo, 0, 0)
         part[1] = dw2 if k == 0 else part[1] + dw2
         src = dx.at[part_rows]
         for to in (2, 4, 1):
@@ -233,12 +235,12 @@
     hbm = pl.BlockSpec(memory_space=pl.ANY)
     return pl.pallas_call(
         exchange_kernel,
-        out_shape=(jax.ShapeDtypeStruct((NDEV * UNIQ, DIM), F32), jax.ShapeDtypeStruct((NDEV, 1, META), jnp.int32), jax.ShapeDtypeStruct((2, DIM, FFN), F32)),
+        out_shape=(jax.ShapeDtypeStruct((NDEV * UNIQ, DIM), F32), jax.ShapeDtypeStruct((NDEV, 1, META), jnp.int32), jax.ShapeDtypeStruct((2, FFN, DIM), F32)),
         in_specs=[vmem] * 5,
         out_specs=(hbm, vmem, hbm),
         scratch_shapes=[
-            pltpu.VMEM((UNIQ, DIM), F32), pltpu.VMEM((2, DIM, FFN), F32), pltpu.VMEM((DIM, FFN), F32), pltpu.VMEM((DIM, FFN), F32),
-            pltpu.VMEM((3, QROWS, FFN), F32), pltpu.VMEM((QROWS, FFN), F32),
+            pltpu.VMEM((UNIQ, DIM), F32), pltpu.VMEM((2, FFN, DIM), F32), pltpu.VMEM((FFN, DIM), F32), pltpu.VMEM((FFN, DIM), F32),
+            pltpu.VMEM((3, QROWS, DIM), F32), pltpu.VMEM((QROWS, DIM), F32),
             pltpu.SemaphoreType.DMA((8, PIECES, 4)), pltpu.SemaphoreType.DMA((8, PIECES)), pltpu.SemaphoreType.DMA((8, 4)), pltpu.SemaphoreType.DMA((8,)),
             pltpu.SemaphoreType.DMA((11,)), pltpu.SemaphoreType.DMA((11,)), pltpu.SemaphoreType.DMA((PIECES + 2,))],
         compiler_params=pltpu.CompilerParams(vmem_limit_bytes=VMEM_LIMIT, collective_id=0, has_side_effects=True),
@@ -246,7 +248,10 @@
     )(x, m, w1, w2, meta)
 
 
-def table_kernel(uid_ref, off_ref, rows_hbm, out_hbm, rows, acc, in_sem, out_sem):
+def table_kernel(meta_hbm, rows_hbm, red_hbm, out_hbm, w1_hbm, w2_hbm, *scratch):
+    meta = scratch[:NDEV]
+    rows, acc, red, meta_sem, in_sem, out_sem, red_sem, w_sem = scratch[NDEV:]
+
     def in_copy(d, half):
         part = pl.ds(d * UNIQ, UNIQ)
         return pltpu.make_async_copy(rows_hbm.at[part, pl.ds(half * 128, 128)], rows.at[half, part], in_sem.at[d, half])
@@ -255,9 +260,16 @@
         part = pl.ds(c * CHUNK, CHUNK if c < NCHUNK - 1 else LAST)
         return pltpu.make_async_copy(acc.at[half, part], out_hbm.at[part, pl.ds(half * 128, 128)], out_sem.at[c, half])
 
+    def meta_copy(d):
+        return pltpu.make_async_copy(meta_hbm.at[d, 0], meta[d], meta_sem.at[d])
+
     for d in range(NDEV):
+        meta_copy(d).start()
+    for d in range(NDEV):
         for half in range(2):
             in_copy(d, half).start()
+    red_in = pltpu.make_async_copy(red_hbm, red, red_sem)
+    red_in.start()
 
     @pl.loop(0, PADDED // ZERO)
     def _(i):
@@ -266,57 +278,66 @@
             acc[half, part] = jnp.zeros((ZERO, 128), F32)
 
     for d in range(NDEV):
+        meta_copy(d).wait()
         for half in range(2):
             in_copy(d, half).wait()
+    red_in.wait()
+    w_out = [pltpu.make_async_copy(red.at[1], w2_hbm, w_sem.at[4])]
+    for q in range(FFN // DIM):
+        w_out.append(pltpu.make_async_copy(red.at[0, pl.ds(q * DIM, DIM)], w1_hbm.at[:, pl.ds(q * DIM, DIM)], w_sem.at[q]))
+    for copy in w_out:
+        copy.start()
 
     for c in range(NCHUNK):
         for d in range(NDEV):
-            first = (off_ref[d * HI + c * CHUNK_HI] + BATCH - 1) // BATCH
-            last = (off_ref[d * HI + (c + 1) * CHUNK_HI] + BATCH - 1) // BATCH if c < NCHUNK - 1 else UNIQ // BATCH
+            first = (meta[d][UNIQ + c * CHUNK_HI] + BATCH - 1) // BATCH if c else 0
+            last = (meta[d][UNIQ + (c + 1) * CHUNK_HI] + BATCH - 1) // BATCH if c < NCHUNK - 1 else UNIQ // BATCH
 
             def fetch(b):
-                base = pl.multiple_of(d * UNIQ + b * BATCH, BATCH)
+                base = pl.multiple_of(b * BATCH, BATCH)
+                at = [meta[d][base + k] for k in range(BATCH)]
                 sums = []
-                for half in range(2):
-                    for k in range(BATCH):
-                        sums.append(acc[half, pl.ds(uid_ref[base + k], 1), :] + rows[half, pl.ds(base + k, 1), :])
-                return sums
-
-            def put(b, sums):
-                base = pl.multiple_of(d * UNIQ + b * BATCH, BATCH)
-                for half in range(2):
-                    for k in range(BATCH):
-                        acc[half, pl.ds(uid_ref[base + k], 1), :] = sums[half * BATCH + k]
-
-            def step(b, sums):
+                for k in range(BATCH):
+                    for half in range(2):
+                        sums.append(acc[half, pl.ds(at[k], 1), :] + rows[half, pl.ds(d * UNIQ + base + k, 1), :])
+                return at, sums
+
+            def put(at, sums):
+                for k in range(BATCH):
+                    for half in range(2):
+                        acc[half, pl.ds(at[k], 1), :] = sums[2 * k + half]
+
+            def step(b, carry):
                 ahead = fetch(b)
-                put(b - 1, sums)
+                put(*carry)
                 return ahead
 
             @pl.when(last > first)
             def _():
-                sums = lax.fori_loop(first + 1, last, step, fetch(first))
-                put(last - 1, sums)
+                put(*lax.fori_loop(first + 1, last, step, fetch(first)))
 
         for half in range(2):
             out_copy(c, half).start()
+    for copy in w_out:
+        copy.wait()
     for c in range(NCHUNK):
         for half in range(2):
             out_copy(c, half).wait()
 
 
-def table(meta, rows):
+def table(meta, rows, red):
+    hbm = pl.BlockSpec(memory_space=pl.ANY)
     return pl.pallas_call(
         table_kernel,
-        grid_spec=pltpu.PrefetchScalarGridSpec(
-            num_scalar_prefetch=2, grid=(1,),
-            in_specs=[pl.BlockSpec(memory_space=pl.ANY)], out_specs=pl.BlockSpec(memory_space=pl.ANY),
-            scratch_shapes=[pltpu.VMEM((2, NDEV * UNIQ, 128), F32), pltpu.VMEM((2, PADDED, 128), F32),
-                            pltpu.SemaphoreType.DMA((NDEV, 2)), pltpu.SemaphoreType.DMA((NCHUNK, 2))]),
-        out_shape=jax.ShapeDtypeStruct((VOCAB, DIM), F32),
+        in_specs=[hbm] * 3, out_specs=(hbm,) * 3,
+        scratch_shapes=[pltpu.SMEM((META,), jnp.int32)] * NDEV + [
+            pltpu.VMEM((2, NDEV * UNIQ, 128), F32), pltpu.VMEM((2, PADDED, 128), F32), pltpu.VMEM((2, FFN, DIM), F32),
+            pltpu.SemaphoreType.DMA((NDEV,)), pltpu.SemaphoreType.DMA((NDEV, 2)), pltpu.SemaphoreType.DMA((NCHUNK, 2)),
+            pltpu.SemaphoreType.DMA, pltpu.SemaphoreType.DMA((5,))],
+        out_shape=(jax.ShapeDtypeStruct((VOCAB, DIM), F32), jax.ShapeDtypeStruct((DIM, FFN), F32), jax.ShapeDtypeStruct((FFN, DIM), F32)),
         compiler_params=pltpu.CompilerParams(vmem_limit_bytes=VMEM_LIMIT),
         name="table",
-    )(meta[:, :UNIQ].reshape(-1), meta[:, UNIQ:].reshape(-1), rows)
+    )(meta, rows, red)
 
 
 def solution(mesh):
@@ -324,6 +345,6 @@
         meta, msum = dedup(n_real, tok_ids.reshape(1, TOK), grad_out)
         x = jnp.take(embed_table, meta[0, :UNIQ], axis=0, mode='clip')
         all_rows, all_meta, red = exchange(x, msum, w_in, w_out, meta)
-        return table(all_meta[:, 0], all_rows), red[0], red[1].T
+        return table(all_meta, all_rows, red)
 
     return jax.shard_map(per_device, mesh=mesh, in_specs=(P('data'), P('data', None), P('data'), P(), P(), P()), out_specs=(P(), P(), P()), check_vma=False)

time: 130 us -> 119 us (0.915)
  local copies, waits for them, and re-layouts: 18.9 us -> 12.9 us
  Pallas kernels: 109 us -> 104 us
    pallas_call x1, Pallas kernels: 30.9 us -> 25.7 us  [table(): pl.pallas_call(table_kernel, in_specs=[hbm] * 3, out_specs=(hbm,) * 3, sc...]
    unnamed x4 -> x0, local copies, waits for them, and re-layouts: 2.71 us -> none
    transpose x1 -> x0, local copies, waits for them, and re-layouts: 2.7 us -> none  [per_device(): return (table(all_meta[:, 0], all_rows), red[0], red[1].T)]
where the time goes in v4:
time: 119 us
  Pallas kernels  104 us (87%)
  local copies, waits for them, and re-layouts  12.9 us (11%)
  between operations  1.45 us (1%)
    pallas_call x1, Pallas kernels, exchange(): pl.pallas_call(exchange_kernel, out_shape=(jax.ShapeDtypeStruct((NDEV * U...  69.2 us
    pallas_call x1, Pallas kernels, table(): pl.pallas_call(table_kernel, in_specs=[hbm] * 3, out_specs=(hbm,) * 3, sc...  25.7 us
    gather x1, local copies, waits for them, and re-layouts, per_device(): x = jnp.take(embed_table, meta[0, :UNIQ], axis=0, mode='clip')  12.2 us
    pallas_call x1, Pallas kernels, dedup(): pl.pallas_call(dedup_kernel, out_shape=(jax.ShapeDtypeStruct((1, META), j...  9.35 us

profile of v4, /device:TPU:0, one launch (start us, length us, event | category | flops | bytes accessed | tf_op | source)
XLA Modules:
  0.0 118.6 jit_solution(5850470429267053655)
XLA Ops:
  1.3 9.3 %dedup.1 = (s32[1,1152]{1,0:T(1,128)}, f32[1024,256]{1,0:T(8,128)}) custom-call(s32[1]{0:T(128)S(6)} %copy.9.n_ref, s32[1,4096]{1,0:T(1,128)} %bitcast.2, bf16[4096,256]{1,0:T(8,128)(2,1)} %dy_ref.1), custom_call_target="tpu_custom_call" | custom-call | tf_op jit(solution)/shard_map/dedup/pallas_call | solution.py:91
  10.6 0.7 slice.3
  11.3 12.2 %gather_fusion = bf16[1024,256]{1,0:T(8,128)(2,1)} fusion(bf16[30522,256]{1,0:T(8,128)(2,1)} %param.9, s32[1024]{0:T(1024)S(1)} %broadcast_clamp_fusion), kind=kCustom, calls=%fused_computation | custom fusion | bytes 1052672 | tf_op jit(solution)/shard_map/jit(_take)/gather | solution.py:346
  23.6 69.2 %exchange.1 = (f32[8192,256]{1,0:T(8,128)}, s32[8,1,1152]{2,1,0:T(1,128)}, f32[2,1024,256]{2,1,0:T(8,128)}) custom-call(bf16[1024,256]{1,0:T(8,128)(2,1)} %gather_fusion, f32[1024,256]{1,0:T(8,128)} %get-tuple-element.9.m_ref, bf16[256,1024]{1,0:T(8,128)(2,1)} %w1_ref.1, bf16[1024,256]{1,0:T(8,128)(2,1)} %w2_ref.1, s32[1,1152]{1,0:T(1,128)} %get-tuple-element.8.meta_ref), custom_call_target="tpu_custom_call" | custom-call | tf_op jit(solution)/shard_map/exchange/pallas_call | solution.py:236
  92.8 25.7 %table.1 = (f32[30522,256]{1,0:T(8,128)}, f32[256,1024]{1,0:T(8,128)}, f32[1024,256]{1,0:T(8,128)}) custom-call(s32[8,1,1152]{2,1,0:T(1,128)} %get-tuple-element.10.meta_hbm, f32[8192,256]{1,0:T(8,128)} %get-tuple-element.11.rows_hbm, f32[2,1024,256]{2,1,0:T(8,128)} %get-tuple-element.12.red_hbm), custom_call_target="tpu_custom_call" | custom-call | tf_op jit(solution)/shard_map/table/pallas_call | solution.py:330
  (1 shorter events, 0.0 us)

commit v5 on v4

--- a/solution.py
+++ b/solution.py
@@ -20,6 +20,8 @@
 HI = 128
 LO = 256
 STEP_TOK = 512
+FETCH = UNIQ * STEP_TOK // TOK
+LAST_TILE = VOCAB // 8 - 1
 CHUNK_HI = 16
 CHUNK = CHUNK_HI * LO
 NCHUNK = -(-VOCAB // CHUNK)
@@ -45,7 +47,7 @@
     return lax.broadcasted_iota(jnp.int32, shape, axis)
 
 
-def dedup_kernel(n_ref, ids_ref, dy_ref, meta_ref, msum_ref):
+def prepare_kernel(n_ref, ids_ref, dy_ref, tail_ref, e_hbm, meta_ref, msum_ref, x_ref, uid, tiles, uid_sem, tile_sem):
     ids = ids_ref[...]
     ohi = (iota((HI, TOK), 0) == (ids >> 8)).astype(BF16)
     olo = (iota((LO, TOK), 0) == (ids & 255)).astype(BF16)
@@ -55,10 +57,6 @@
     total = dot(present, jnp.ones((LO, UNIQ), BF16), 1, 0)
     lower = (iota((HI, HI), 1) < iota((HI, HI), 0)).astype(BF16)
     offset = dot(lower, total.astype(BF16), 1, 0)
-    rank = before + offset[:, :LO]
-    rank_a = jnp.floor(rank * (1.0 / 32.0))
-    rank_b = (rank - 32.0 * rank_a).astype(BF16)
-    rank_a = rank_a.astype(BF16)
 
     lane = iota((HI, UNIQ), 1).astype(F32)
     hi_of = jnp.sum(((offset + total) <= lane).astype(F32), axis=0, keepdims=True)
@@ -67,35 +65,66 @@
     upto = (before + present.astype(F32)).astype(BF16)
     row_of = dot(upto, hot.astype(BF16), 0, 0)
     lo_of = jnp.sum((row_of <= k_of).astype(F32), axis=0, keepdims=True)
-    meta_ref[:, :UNIQ] = (hi_of * 256.0 + lo_of).astype(jnp.int32)
+    uid_row = (hi_of * 256.0 + lo_of).astype(jnp.int32)
+    meta_ref[:, :UNIQ] = uid_row
     eye = iota((HI, HI), 0) == iota((HI, HI), 1)
     meta_ref[:, UNIQ:] = jnp.sum(jnp.where(eye, offset[:, :HI], 0.0), axis=0, keepdims=True).astype(jnp.int32)
-
+    to_smem = pltpu.make_async_copy(meta_ref.at[0], uid, uid_sem)
+    to_smem.start()
+
+    rank = before + offset[:, :LO]
+    rank_a = jnp.floor(rank * (1.0 / 32.0))
+    rank_b = (rank - 32.0 * rank_a).astype(BF16)
+    rank_a = rank_a.astype(BF16)
+    msum_ref[...] = jnp.zeros((UNIQ, DIM), F32)
     kept = n_ref[0]
-    for b in range(TOK // STEP_TOK):
-        cols = slice(b * STEP_TOK, (b + 1) * STEP_TOK)
-        mine = ohi[:, cols]
-        pos = 32.0 * dot(rank_a, mine, 0, 0) + dot(rank_b, mine, 0, 0)
-        slot = jnp.sum(pos * olo[:, cols].astype(F32), axis=0, keepdims=True)
+    to_smem.wait()
+
+    def step(b, carry):
+        for j in range(FETCH):
+            at = b * FETCH + j
+            tile = jnp.minimum(uid[at] >> 3, LAST_TILE)
+            pltpu.make_async_copy(e_hbm.at[pl.ds(pl.multiple_of(tile * 8, 8), 8)], tiles.at[pl.ds(pl.multiple_of(at * 8, 8), 8)], tile_sem).start()
+        cols = pl.ds(pl.multiple_of(b * STEP_TOK, STEP_TOK), STEP_TOK)
+        mine = ids_ref[:, cols]
+        mine_hi = (iota((HI, STEP_TOK), 0) == (mine >> 8)).astype(BF16)
+        pos = 32.0 * dot(rank_a, mine_hi, 0, 0) + dot(rank_b, mine_hi, 0, 0)
+        slot = jnp.sum(jnp.where(iota((LO, STEP_TOK), 0) == (mine & 255), pos, 0.0), axis=0, keepdims=True)
         tok = iota((1, STEP_TOK), 1) + b * STEP_TOK
         slot = jnp.where(tok < kept, slot.astype(jnp.int32), -1)
         pick = (iota((UNIQ, STEP_TOK), 0) == slot).astype(BF16)
-        part = dot(pick, dy_ref[cols, :], 1, 0)
-        if b == 0:
-            msum_ref[...] = part
-        else:
-            msum_ref[...] += part
-
-
-def dedup(n_real, ids, dy):
+        msum_ref[...] += dot(pick, dy_ref[cols, :], 1, 0)
+        return carry
+
+    lax.fori_loop(0, TOK // STEP_TOK, step, 0)
+    pltpu.make_async_copy(tiles, tiles, tile_sem).wait()
+
+    uid_col = jnp.broadcast_to(uid_row.astype(F32), (128, UNIQ)).T.astype(jnp.int32)
+    place = (uid_col & 7) + 8 * (iota((UNIQ, 128), 0) & 31)
+    for g in range(UNIQ // 32):
+        want = place[g * 32:(g + 1) * 32]
+        lanes = iota((32, 128), 1)
+        pick = jnp.concatenate([(want == lanes).astype(BF16), (want == lanes + 128).astype(BF16)], axis=1)
+        x_ref[pl.ds(g * 32, 32), :] = dot(pick, tiles[pl.ds(g * 256, 256), :], 1, 0).astype(BF16)
+
+    uid_two = jnp.concatenate([uid_col, uid_col], axis=1)
+    x = x_ref[...]
+    for r in range(VOCAB - 8 * (LAST_TILE + 1)):
+        x = jnp.where(uid_two == 8 * (LAST_TILE + 1) + r, tail_ref[pl.ds(r, 1), :].astype(F32), x.astype(F32)).astype(BF16)
+    x_ref[...] = x
+
+
+def prepare(n_real, ids, dy, table, tail):
+    vmem = pl.BlockSpec(memory_space=pltpu.VMEM)
     return pl.pallas_call(
-        dedup_kernel,
-        out_shape=(jax.ShapeDtypeStruct((1, META), jnp.int32), jax.ShapeDtypeStruct((UNIQ, DIM), F32)),
-        in_specs=[pl.BlockSpec(memory_space=pltpu.SMEM), pl.BlockSpec(memory_space=pltpu.VMEM), pl.BlockSpec(memory_space=pltpu.VMEM)],
-        out_specs=(pl.BlockSpec(memory_space=pltpu.VMEM), pl.BlockSpec(memory_space=pltpu.VMEM)),
+        prepare_kernel,
+        out_shape=(jax.ShapeDtypeStruct((1, META), jnp.int32), jax.ShapeDtypeStruct((UNIQ, DIM), F32), jax.ShapeDtypeStruct((UNIQ, DIM), BF16)),
+        in_specs=[pl.BlockSpec(memory_space=pltpu.SMEM), vmem, vmem, vmem, pl.BlockSpec(memory_space=pl.ANY)],
+        out_specs=(vmem, vmem, vmem),
+        scratch_shapes=[pltpu.SMEM((META,), jnp.int32), pltpu.VMEM((8 * UNIQ, DIM), BF16), pltpu.SemaphoreType.DMA, pltpu.SemaphoreType.DMA],
         compiler_params=pltpu.CompilerParams(vmem_limit_bytes=VMEM_LIMIT),
-        name="dedup",
-    )(n_real, ids, dy)
+        name="prepare",
+    )(n_real, ids, dy, tail, table)
 
 
 def exchange_kernel(x_ref, m_ref, w1_ref, w2_ref, meta_ref, rows_ref, meta_out, red_ref,
@@ -293,14 +322,12 @@
             first = (meta[d][UNIQ + c * CHUNK_HI] + BATCH - 1) // BATCH if c else 0
             last = (meta[d][UNIQ + (c + 1) * CHUNK_HI] + BATCH - 1) // BATCH if c < NCHUNK - 1 else UNIQ // BATCH
 
-            def fetch(b):
+            def read(b):
+                return [meta[d][b * BATCH + k] for k in range(BATCH)]
+
+            def fetch(b, at):
                 base = pl.multiple_of(b * BATCH, BATCH)
-                at = [meta[d][base + k] for k in range(BATCH)]
-                sums = []
-                for k in range(BATCH):
-                    for half in range(2):
-                        sums.append(acc[half, pl.ds(at[k], 1), :] + rows[half, pl.ds(d * UNIQ + base + k, 1), :])
-                return at, sums
+                return [acc[half, pl.ds(at[k], 1), :] + rows[half, pl.ds(d * UNIQ + base + k, 1), :] for k in range(BATCH) for half in range(2)]
 
             def put(at, sums):
                 for k in range(BATCH):
@@ -308,13 +335,17 @@
                         acc[half, pl.ds(at[k], 1), :] = sums[2 * k + half]
 
             def step(b, carry):
-                ahead = fetch(b)
-                put(*carry)
-                return ahead
+                at_new, at_old, sums_old = carry
+                sums_new = fetch(b, at_new)
+                at_next = read(b + 1)
+                put(at_old, sums_old)
+                return at_next, at_new, sums_new
 
             @pl.when(last > first)
             def _():
-                put(*lax.fori_loop(first + 1, last, step, fetch(first)))
+                at = read(first)
+                _, at, sums = lax.fori_loop(first + 1, last, step, (read(first + 1), at, fetch(first, at)))
+                put(at, sums)
 
         for half in range(2):
             out_copy(c, half).start()
@@ -342,8 +373,8 @@
 
 def solution(mesh):
     def per_device(tok_ids, grad_out, n_real, embed_table, w_in, w_out):
-        meta, msum = dedup(n_real, tok_ids.reshape(1, TOK), grad_out)
-        x = jnp.take(embed_table, meta[0, :UNIQ], axis=0, mode='clip')
+        tail = embed_table[8 * (LAST_TILE + 1):].astype(F32)
+        meta, msum, x = prepare(n_real, tok_ids.reshape(1, TOK), grad_out, embed_table, tail)
         all_rows, all_meta, red = exchange(x, msum, w_in, w_out, meta)
         return table(all_meta, all_rows, red)
 

time: 119 us -> 113 us (0.950)
  local copies, waits for them, and re-layouts: 12.9 us -> 0 us
  Pallas kernels: 104 us -> 111 us
  other arithmetic: 0.01 us -> 1.25 us
    gather x1 -> x0, local copies, waits for them, and re-layouts: 12.2 us -> none  [per_device(): x = jnp.take(embed_table, meta[0, :UNIQ], axis=0, mode='clip')]
    pallas_call x1, Pallas kernels: 9.35 us -> 13.6 us  [prepare(): pl.pallas_call(prepare_kernel, out_shape=(jax.ShapeDtypeStruct((1, META),...]
    pallas_call x1, Pallas kernels: 25.7 us -> 28 us  [table(): pl.pallas_call(table_kernel, in_specs=[hbm] * 3, out_specs=(hbm,) * 3, sc...]
    convert_element_type x0 -> x1, other arithmetic: none -> 1.25 us  [per_device(): tail = embed_table[8 * (LAST_TILE + 1):].astype(F32)]
where the time goes in v5:
time: 113 us
  Pallas kernels  111 us (98%)
  between operations  1.29 us (1%)
  other arithmetic  1.25 us (1%)
    pallas_call x1, Pallas kernels, exchange(): pl.pallas_call(exchange_kernel, out_shape=(jax.ShapeDtypeStruct((NDEV * U...  69.2 us
    pallas_call x1, Pallas kernels, table(): pl.pallas_call(table_kernel, in_specs=[hbm] * 3, out_specs=(hbm,) * 3, sc...  28 us
    pallas_call x1, Pallas kernels, prepare(): pl.pallas_call(prepare_kernel, out_shape=(jax.ShapeDtypeStruct((1, META),...  13.6 us

profile of v5, /device:TPU:0, one launch (start us, length us, event | category | flops | bytes accessed | tf_op | source)
XLA Modules:
  0.0 113.3 jit_solution(542580171391915299)
XLA Ops:
  1.3 1.3 %slice_convert_fusion.tail_ref = f32[2,256]{1,0:T(2,128)} fusion(bf16[30522,256]{1,0:T(8,128)(2,1)} %e_hbm.1), kind=kLoop, calls=%fused_computation | loop fusion | flops 512 | bytes 3072 | tf_op jit(solution)/shard_map/convert_element_type | solution.py:376
  2.5 13.6 %prepare.1 = (s32[1,1152]{1,0:T(1,128)}, f32[1024,256]{1,0:T(8,128)}, bf16[1024,256]{1,0:T(8,128)(2,1)}) custom-call(s32[1]{0:T(128)S(6)} %copy.9.n_ref, s32[1,4096]{1,0:T(1,128)} %bitcast.1, bf16[4096,256]{1,0:T(8,128)(2,1)} %dy_ref.1, f32[2,256]{1,0:T(2,128)} %slice_convert_fusion.tail_ref, bf16[30522,256]{1,0:T(8,128)(2,1)} %e_hbm.1), custom_call_target="tpu_custom_call" | custom-call | tf_op jit(solution)/shard_map/prepare/pallas_call | solution.py:119
  16.1 69.2 %exchange.1 = (f32[8192,256]{1,0:T(8,128)}, s32[8,1,1152]{2,1,0:T(1,128)}, f32[2,1024,256]{2,1,0:T(8,128)}) custom-call(bf16[1024,256]{1,0:T(8,128)(2,1)} %get-tuple-element.9.x_ref, f32[1024,256]{1,0:T(8,128)} %get-tuple-element.10.m_ref, bf16[256,1024]{1,0:T(8,128)(2,1)} %w1_ref.1, bf16[1024,256]{1,0:T(8,128)(2,1)} %w2_ref.1, ...), custom_call_target="tpu_custom_call" | custom-call | tf_op jit(solution)/shard_map/exchange/pallas_call | solution.py:265
  85.3 28.0 %table.1 = (f32[30522,256]{1,0:T(8,128)}, f32[256,1024]{1,0:T(8,128)}, f32[1024,256]{1,0:T(8,128)}) custom-call(s32[8,1,1152]{2,1,0:T(1,128)} %get-tuple-element.12.meta_hbm, f32[8192,256]{1,0:T(8,128)} %get-tuple-element.13.rows_hbm, f32[2,1024,256]{2,1,0:T(8,128)} %get-tuple-element.14.red_hbm), custom_call_target="tpu_custom_call" | custom-call | tf_op jit(solution)/shard_map/table/pallas_call | solution.py:361

commit v6 on v5

--- a/solution.py
+++ b/solution.py
@@ -31,7 +31,7 @@
 ZERO = 192
 PIECES = 4
 PIECE = UNIQ // PIECES
-QROWS = FFN // 4
+EIGHTH = FFN // 8
 META = UNIQ + HI
 
 F32 = jnp.float32
@@ -128,7 +128,7 @@
 
 
 def exchange_kernel(x_ref, m_ref, w1_ref, w2_ref, meta_ref, rows_ref, meta_out, red_ref,
-                    dx, part, pin, chip, rs, fin, row_send, row_recv, meta_send, meta_recv, w_send, w_recv, own_sem):
+                    dx, part, pin, chip, first_in, two, second_in, fin, row_send, row_recv, meta_send, meta_recv, w_send, w_recv, own_sem):
     me = lax.axis_index('data')
     core, px, py = me % 2, (me // 2) % 2, me // 4
 
@@ -171,7 +171,7 @@
     for to in (1, 2, 4, 6):
         send_meta(0, to)
 
-    for k in range(PIECES):
+    def compute(k):
         part_rows = pl.ds(k * PIECE, PIECE)
         x = x_ref[part_rows, :]
         m = m_ref[part_rows, :]
@@ -190,69 +190,111 @@
             part[0, cols] = dw1 if k == 0 else part[0, cols] + dw1
         dw2 = dot(h, m_hi, 0, 0) + dot(h, m_lo, 0, 0)
         part[1] = dw2 if k == 0 else part[1] + dw2
-        src = dx.at[part_rows]
-        for to in (2, 4, 1):
-            send_rows(0, k, to, src)
-        copy = pltpu.make_async_copy(src, rows_at(0, k), own_sem.at[k])
+        copy = pltpu.make_async_copy(dx.at[part_rows], rows_at(0, k), own_sem.at[k])
         copy.start()
         own.append(copy)
+
+    def send_own(k, *tos):
+        for to in tos:
+            send_rows(0, k, to, dx.at[pl.ds(k * PIECE, PIECE)])
 
     def w_copy(src, dst, i, to):
         copy = remote(src, dst, w_send.at[i], w_recv.at[i], to)
         copy.start()
         sent.append(copy)
 
-    def quarter(r):
-        return pl.ds(pl.multiple_of((dev(r) // 2) * QROWS, QROWS), QROWS)
-
+    def w_got(dst, i):
+        remote(dst, dst, w_send.at[i], w_recv.at[i], 1).wait_recv()
+
+    def forward(k):
+        got_rows(2, k)
+        if k % 2 == 0:
+            send_rows(2, k, 4)
+        send_rows(2, k, 1)
+        got_rows(4, k)
+        if k % 2 == 1:
+            send_rows(4, k, 2)
+        send_rows(4, k, 1)
+
+    def eighth(half, a, b):
+        return pl.ds(pl.multiple_of((half * 4 + a * 2 + b) * EIGHTH, EIGHTH), EIGHTH)
+
+    def pair(half, a):
+        return pl.ds(pl.multiple_of((half * 4 + a * 2) * EIGHTH, 2 * EIGHTH), 2 * EIGHTH)
+
+    def red_at(half, flip_x, flip_y, flip_core=0):
+        ax = px + flip_x * (1 - 2 * px)
+        ay = py + flip_y * (1 - 2 * py)
+        a, b = (ax, ay) if half == 0 else (ay, ax)
+        return red_ref.at[(core + flip_core) % 2, eighth(half, a, b)]
+
+    compute(0)
+    send_own(0, 2, 4, 1)
+    compute(1)
+    send_own(1, 2, 4, 1)
+    compute(2)
+    compute(3)
     w_copy(part.at[1 - core], pin, 0, 1)
-    remote(pin, pin, w_send.at[0], w_recv.at[0], 1).wait_recv()
+    send_own(2, 1)
+    send_own(3, 1)
+    w_got(pin, 0)
     chip[...] = part[core] + pin[...]
-    for i, to in enumerate((2, 4, 6)):
-        w_copy(chip.at[quarter(to)], rs.at[i], 1 + i, to)
+    w_copy(chip.at[pair(0, 1 - px)], first_in.at[0], 1, 2)
+    w_copy(chip.at[pair(1, 1 - py)], first_in.at[1], 2, 4)
+    send_own(2, 2, 4)
 
     for block in (2, 4, 6):
         got_meta(block)
         send_meta(block, 1)
-
-    for k in range(PIECES):
-        got_rows(2, k)
-        if k < PIECES // 2:
-            send_rows(2, k, 4)
-        send_rows(2, k, 1)
-        got_rows(4, k)
-        if k >= PIECES // 2:
-            send_rows(4, k, 2)
-        send_rows(4, k, 1)
-
-    for i, to in enumerate((2, 4, 6)):
-        remote(rs.at[i], rs.at[i], w_send.at[1 + i], w_recv.at[1 + i], to).wait_recv()
-    fin[...] = (chip[quarter(0), :] + rs[0]) + (rs[1] + rs[2])
-
-    def red_at(r):
-        return red_ref.at[(core + r) % 2, quarter(r)]
-
-    for i, to in enumerate((2, 4, 6)):
-        w_copy(fin, red_at(0), 4 + i, to)
-    w_copy(fin, red_at(0), 7, 1)
-    copy = pltpu.make_async_copy(fin, red_at(0), own_sem.at[PIECES + 1])
-    copy.start()
-    own.append(copy)
-
+    forward(0)
+
+    w_got(first_in.at[0], 1)
+    two[0] = chip[pair(0, px), :] + first_in[0]
+    w_copy(two.at[0, pl.ds(pl.multiple_of((1 - py) * EIGHTH, EIGHTH), EIGHTH)], second_in.at[0], 3, 4)
+    w_got(first_in.at[1], 2)
+    two[1] = chip[pair(1, py), :] + first_in[1]
+    w_copy(two.at[1, pl.ds(pl.multiple_of((1 - px) * EIGHTH, EIGHTH), EIGHTH)], second_in.at[1], 4, 2)
+    send_own(3, 2, 4)
+    forward(1)
+
+    w_got(second_in.at[0], 3)
+    fin[0] = two[0, pl.ds(pl.multiple_of(py * EIGHTH, EIGHTH), EIGHTH), :] + second_in[0]
+    w_got(second_in.at[1], 4)
+    fin[1] = two[1, pl.ds(pl.multiple_of(px * EIGHTH, EIGHTH), EIGHTH), :] + second_in[1]
+    for half in range(2):
+        w_copy(fin.at[half], red_at(half, 0, 0), 5 + half, 2)
+        w_copy(fin.at[half], red_at(half, 0, 0), 7 + half, 4)
+        w_copy(fin.at[half], red_at(half, 0, 0), 11 + half, 1)
+        copy = pltpu.make_async_copy(fin.at[half], red_at(half, 0, 0), own_sem.at[PIECES + 1 + half])
+        copy.start()
+        own.append(copy)
+    forward(2)
+
+    w_got(red_at(0, 0, 1), 7)
+    w_copy(red_at(0, 0, 1), red_at(0, 0, 1), 9, 2)
+    w_copy(red_at(0, 0, 1), red_at(0, 0, 1), 13, 1)
+    w_got(red_at(1, 1, 0), 6)
+    w_copy(red_at(1, 1, 0), red_at(1, 1, 0), 10, 4)
+    w_copy(red_at(1, 1, 0), red_at(1, 1, 0), 14, 1)
+    w_got(red_at(0, 1, 0), 5)
+    w_copy(red_at(0, 1, 0), red_at(0, 1, 0), 15, 1)
+    w_got(red_at(1, 0, 1), 8)
+    w_copy(red_at(1, 0, 1), red_at(1, 0, 1), 16, 1)
+    forward(3)
+
+    for half in range(2):
+        w_got(red_at(half, 1, 1), 9 + half)
+        w_copy(red_at(half, 1, 1), red_at(half, 1, 1), 17 + half, 1)
     for k in range(PIECES):
         got_rows(6, k)
         send_rows(6, k, 1)
 
-    for i, block in enumerate((2, 4, 6)):
-        remote(red_at(block), red_at(block), w_send.at[4 + i], w_recv.at[4 + i], 1).wait_recv()
-        w_copy(red_at(block), red_at(block), 8 + i, 1)
-
+    for i, (half, fx, fy) in enumerate(((0, 0, 0), (1, 0, 0), (0, 0, 1), (1, 1, 0), (0, 1, 0), (1, 0, 1), (0, 1, 1), (1, 1, 1))):
+        w_got(red_at(half, fx, fy, 1), 11 + i)
     for block in (1, 3, 5, 7):
         got_meta(block)
         for k in range(PIECES):
             got_rows(block, k)
-    for i, block in enumerate((1, 3, 5, 7)):
-        remote(red_at(block), red_at(block), w_send.at[7 + i], w_recv.at[7 + i], 1).wait_recv()
     for copy in sent:
         copy.wait_send()
     for copy in own:
@@ -269,9 +311,9 @@
         out_specs=(hbm, vmem, hbm),
         scratch_shapes=[
             pltpu.VMEM((UNIQ, DIM), F32), pltpu.VMEM((2, FFN, DIM), F32), pltpu.VMEM((FFN, DIM), F32), pltpu.VMEM((FFN, DIM), F32),
-            pltpu.VMEM((3, QROWS, DIM), F32), pltpu.VMEM((QROWS, DIM), F32),
+            pltpu.VMEM((2, 2 * EIGHTH, DIM), F32), pltpu.VMEM((2, 2 * EIGHTH, DIM), F32), pltpu.VMEM((2, EIGHTH, DIM), F32), pltpu.VMEM((2, EIGHTH, DIM), F32),
             pltpu.SemaphoreType.DMA((8, PIECES, 4)), pltpu.SemaphoreType.DMA((8, PIECES)), pltpu.SemaphoreType.DMA((8, 4)), pltpu.SemaphoreType.DMA((8,)),
-            pltpu.SemaphoreType.DMA((11,)), pltpu.SemaphoreType.DMA((11,)), pltpu.SemaphoreType.DMA((PIECES + 2,))],
+            pltpu.SemaphoreType.DMA((19,)), pltpu.SemaphoreType.DMA((19,)), pltpu.SemaphoreType.DMA((PIECES + 3,))],
         compiler_params=pltpu.CompilerParams(vmem_limit_bytes=VMEM_LIMIT, collective_id=0, has_side_effects=True),
         name="exchange",
     )(x, m, w1, w2, meta)
@@ -322,12 +364,14 @@
             first = (meta[d][UNIQ + c * CHUNK_HI] + BATCH - 1) // BATCH if c else 0
             last = (meta[d][UNIQ + (c + 1) * CHUNK_HI] + BATCH - 1) // BATCH if c < NCHUNK - 1 else UNIQ // BATCH
 
-            def read(b):
-                return [meta[d][b * BATCH + k] for k in range(BATCH)]
-
-            def fetch(b, at):
+            def fetch(b):
                 base = pl.multiple_of(b * BATCH, BATCH)
-                return [acc[half, pl.ds(at[k], 1), :] + rows[half, pl.ds(d * UNIQ + base + k, 1), :] for k in range(BATCH) for half in range(2)]
+                at = [meta[d][base + k] for k in range(BATCH)]
+                sums = []
+                for k in range(BATCH):
+                    for half in range(2):
+                        sums.append(acc[half, pl.ds(at[k], 1), :] + rows[half, pl.ds(d * UNIQ + base + k, 1), :])
+                return at, sums
 
             def put(at, sums):
                 for k in range(BATCH):
@@ -335,17 +379,13 @@
                         acc[half, pl.ds(at[k], 1), :] = sums[2 * k + half]
 
             def step(b, carry):
-                at_new, at_old, sums_old = carry
-                sums_new = fetch(b, at_new)
-                at_next = read(b + 1)
-                put(at_old, sums_old)
-                return at_next, at_new, sums_new
+                ahead = fetch(b)
+                put(*carry)
+                return ahead
 
             @pl.when(last > first)
             def _():
-                at = read(first)
-                _, at, sums = lax.fori_loop(first + 1, last, step, (read(first + 1), at, fetch(first, at)))
-                put(at, sums)
+                put(*lax.fori_loop(first + 1, last, step, fetch(first)))
 
         for half in range(2):
             out_copy(c, half).start()

time: 113 us -> 107 us (0.947)
  Pallas kernels: 111 us -> 104 us
    pallas_call x1, Pallas kernels: 69.2 us -> 64.4 us  [exchange(): pl.pallas_call(exchange_kernel, out_shape=(jax.ShapeDtypeStruct((NDEV * U...]
    pallas_call x1, Pallas kernels: 28 us -> 25.8 us  [table(): pl.pallas_call(table_kernel, in_specs=[hbm] * 3, out_specs=(hbm,) * 3, sc...]
where the time goes in v6:
time: 107 us; the launch traced here: 106 us
  Pallas kernels  104 us (97%)
  between operations  1.29 us (1%)
  other arithmetic  1.25 us (1%)
    pallas_call x1, Pallas kernels, exchange(): pl.pallas_call(exchange_kernel, out_shape=(jax.ShapeDtypeStruct((NDEV * U...  64.4 us
    pallas_call x1, Pallas kernels, table(): pl.pallas_call(table_kernel, in_specs=[hbm] * 3, out_specs=(hbm,) * 3, sc...  25.8 us
    pallas_call x1, Pallas kernels, prepare(): pl.pallas_call(prepare_kernel, out_shape=(jax.ShapeDtypeStruct((1, META),...  13.6 us

profile of v6, /device:TPU:0, one launch (start us, length us, event | category | flops | bytes accessed | tf_op | source)
XLA Modules:
  0.0 106.3 jit_solution(4476701037648859374)
XLA Ops:
  1.3 1.3 %slice_convert_fusion.tail_ref = f32[2,256]{1,0:T(2,128)} fusion(bf16[30522,256]{1,0:T(8,128)(2,1)} %e_hbm.1), kind=kLoop, calls=%fused_computation | loop fusion | flops 512 | bytes 3072 | tf_op jit(solution)/shard_map/convert_element_type | solution.py:416
  2.5 13.6 %prepare.1 = (s32[1,1152]{1,0:T(1,128)}, f32[1024,256]{1,0:T(8,128)}, bf16[1024,256]{1,0:T(8,128)(2,1)}) custom-call(s32[1]{0:T(128)S(6)} %copy.9.n_ref, s32[1,4096]{1,0:T(1,128)} %bitcast.1, bf16[4096,256]{1,0:T(8,128)(2,1)} %dy_ref.1, f32[2,256]{1,0:T(2,128)} %slice_convert_fusion.tail_ref, bf16[30522,256]{1,0:T(8,128)(2,1)} %e_hbm.1), custom_call_target="tpu_custom_call" | custom-call | tf_op jit(solution)/shard_map/prepare/pallas_call | solution.py:119
  16.1 64.4 %exchange.1 = (f32[8192,256]{1,0:T(8,128)}, s32[8,1,1152]{2,1,0:T(1,128)}, f32[2,1024,256]{2,1,0:T(8,128)}) custom-call(bf16[1024,256]{1,0:T(8,128)(2,1)} %get-tuple-element.9.x_ref, f32[1024,256]{1,0:T(8,128)} %get-tuple-element.10.m_ref, bf16[256,1024]{1,0:T(8,128)(2,1)} %w1_ref.1, bf16[1024,256]{1,0:T(8,128)(2,1)} %w2_ref.1, ...), custom_call_target="tpu_custom_call" | custom-call | tf_op jit(solution)/shard_map/exchange/pallas_call | solution.py:307
  80.6 25.8 %table.1 = (f32[30522,256]{1,0:T(8,128)}, f32[256,1024]{1,0:T(8,128)}, f32[1024,256]{1,0:T(8,128)}) custom-call(s32[8,1,1152]{2,1,0:T(1,128)} %get-tuple-element.12.meta_hbm, f32[8192,256]{1,0:T(8,128)} %get-tuple-element.13.rows_hbm, f32[2,1024,256]{2,1,0:T(8,128)} %get-tuple-element.14.red_hbm), custom_call_target="tpu_custom_call" | custom-call | tf_op jit(solution)/shard_map/table/pallas_call | solution.py:401

commit v7 on v4

v7 whole, which is shorter than its diff:
```python
import functools
import math

import jax
import jax.numpy as jnp
from jax import lax
from jax.experimental import pallas as pl
from jax.experimental.pallas import tpu as pltpu
from jax.sharding import PartitionSpec as P

GELU_A = 0.044715
GELU_C = math.sqrt(2.0 / math.pi)

NDEV = 8
TOK = 4096
VOCAB = 30522
DIM = 256
FFN = 1024
UNIQ = 1024
HI = 128
LO = 256
STEP_TOK = 512
CHUNK_HI = 16
CHUNK = CHUNK_HI * LO
NCHUNK = -(-VOCAB // CHUNK)
LAST = VOCAB - (NCHUNK - 1) * CHUNK
BATCH = 8
PADDED = 30528
ZERO = 192
PIECES = 4
PIECE = UNIQ // PIECES
ESTEP = 2176
EBLOCK = 128
NESTEP = VOCAB // ESTEP
ETAIL = -(-(VOCAB - NESTEP * ESTEP) // 8) * 8
META = UNIQ + HI

F32 = jnp.float32
BF16 = jnp.bfloat16
VMEM_LIMIT = 62 * 1024 * 1024
VMEM_LIMIT_MAX = 67043328


def dot(a, b, ca, cb):
    return lax.dot_general(a, b, (((ca,), (cb,)), ((), ())), preferred_element_type=F32)


def iota(shape, axis):
    return lax.broadcasted_iota(jnp.int32, shape, axis)


def prepare_kernel(n_ref, ids_ref, dy_ref, meta_ref, msum_ref):
    ids = ids_ref[...]
    ohi = (iota((HI, TOK), 0) == (ids >> 8)).astype(BF16)
    olo = (iota((LO, TOK), 0) == (ids & 255)).astype(BF16)
    present = (dot(ohi, olo, 1, 1) > 0.5).astype(BF16)
    upper = (iota((LO, LO), 0) < iota((LO, LO), 1)).astype(BF16)
    before = dot(present, upper, 1, 0)
    total = dot(present, jnp.ones((LO, UNIQ), BF16), 1, 0)
    lower = (iota((HI, HI), 1) < iota((HI, HI), 0)).astype(BF16)
    offset = dot(lower, total.astype(BF16), 1, 0)

    lane = iota((HI, UNIQ), 1).astype(F32)
    hi_of = jnp.sum(((offset + total) <= lane).astype(F32), axis=0, keepdims=True)
    hot = iota((HI, UNIQ), 0).astype(F32) == hi_of
    k_of = lane[:1] - jnp.sum(jnp.where(hot, offset, 0.0), axis=0, keepdims=True)
    upto = (before + present.astype(F32)).astype(BF16)
    row_of = dot(upto, hot.astype(BF16), 0, 0)
    lo_of = jnp.sum((row_of <= k_of).astype(F32), axis=0, keepdims=True)
    uid_row = (hi_of * 256.0 + lo_of).astype(jnp.int32)
    meta_ref[:, :UNIQ] = uid_row
    eye = iota((HI, HI), 0) == iota((HI, HI), 1)
    meta_ref[:, UNIQ:] = jnp.sum(jnp.where(eye, offset[:, :HI], 0.0), axis=0, keepdims=True).astype(jnp.int32)

    rank = before + offset[:, :LO]
    rank_a = jnp.floor(rank * (1.0 / 32.0))
    rank_b = (rank - 32.0 * rank_a).astype(BF16)
    rank_a = rank_a.astype(BF16)
    msum_ref[...] = jnp.zeros((UNIQ, DIM), F32)
    kept = n_ref[0]

    def step(b, carry):
        cols = pl.ds(pl.multiple_of(b * STEP_TOK, STEP_TOK), STEP_TOK)
        mine = ids_ref[:, cols]
        mine_hi = (iota((HI, STEP_TOK), 0) == (mine >> 8)).astype(BF16)
        pos = 32.0 * dot(rank_a, mine_hi, 0, 0) + dot(rank_b, mine_hi, 0, 0)
        slot = jnp.sum(jnp.where(iota((LO, STEP_TOK), 0) == (mine & 255), pos, 0.0), axis=0, keepdims=True)
        tok = iota((1, STEP_TOK), 1) + b * STEP_TOK
        slot = jnp.where(tok < kept, slot.astype(jnp.int32), -1)
        pick = (iota((UNIQ, STEP_TOK), 0) == slot).astype(BF16)
        msum_ref[...] += dot(pick, dy_ref[cols, :], 1, 0)
        return carry

    lax.fori_loop(0, TOK // STEP_TOK, step, 0)


def prepare(n_real, ids, dy):
    vmem = pl.BlockSpec(memory_space=pltpu.VMEM)
    return pl.pallas_call(
        prepare_kernel,
        out_shape=(jax.ShapeDtypeStruct((1, META), jnp.int32), jax.ShapeDtypeStruct((UNIQ, DIM), F32)),
        in_specs=[pl.BlockSpec(memory_space=pltpu.SMEM), vmem, vmem],
        out_specs=(vmem, vmem),
        compiler_params=pltpu.CompilerParams(vmem_limit_bytes=VMEM_LIMIT),
        name="prepare",
    )(n_real, ids, dy)


def exchange_kernel(m_hbm, w1_ref, w2_ref, meta_ref, tail_ref, e_hbm, rows_ref, meta_out, red_ref,
                    e_wide, stage, all_m, x_wide, dx, part, pin, uid,
                    stage_sem, own_sem, uid_sem, m_send, m_recv, meta_send, meta_recv, dx_send, dx_recv, dx_own, w_send, w_recv):
    me = lax.axis_index('data')
    core, px, py = me % 2, (me // 2) % 2, me // 4

    def dev(r):
        return me + (r % 2) * (1 - 2 * core) + ((r // 2) % 2) * (2 - 4 * px) + (r // 4) * (4 - 8 * py)

    def remote(src, dst, send, recv, r):
        return pltpu.make_async_remote_copy(src_ref=src, dst_ref=dst, send_sem=send, recv_sem=recv, device_id=(dev(r),), device_id_type=pl.DeviceIdType.MESH)

    def piece(k):
        return pl.ds(pl.multiple_of(k * PIECE, PIECE), PIECE)

    def stage_copy(c):
        return pltpu.make_async_copy(e_hbm.at[pl.ds(c * ESTEP, ESTEP)], stage.at[c % 2], stage_sem.at[c % 2])

    own_m = pltpu.make_async_copy(m_hbm, all_m.at[0], own_sem.at[0])
    own_m.start()
    stage_copy(0).start()
    stage_copy(1).start()
    own_meta = pltpu.make_async_copy(meta_ref, meta_out.at[me], own_sem.at[1])
    own_meta.start()

    barrier = pltpu.get_barrier_semaphore()
    for r in (1, 2, 4, 6):
        pl.semaphore_signal(barrier, inc=1, device_id=(dev(r),), device_id_type=pl.DeviceIdType.MESH)
    pl.semaphore_wait(barrier, 4)

    sent = []

    def send_meta(block, to):
        src = meta_ref if block == 0 else meta_out.at[dev(block)]
        copy = remote(src, meta_out.at[dev(block)], meta_send.at[block, to // 2], meta_recv.at[block ^ to], to)
        copy.start()
        sent.append(copy)

    def got_meta(block):
        at = meta_out.at[dev(block)]
        remote(at, at, meta_send.at[block, 0], meta_recv.at[block], 1).wait_recv()

    for to in (2, 4, 6, 1):
        send_meta(0, to)
    for k in range(PIECES):
        for to in (2, 4):
            copy = remote(m_hbm.at[piece(k)], all_m.at[to // 2, piece(k)], m_send.at[to // 2 - 1, k], m_recv.at[to // 2, k], to)
            copy.start()
            sent.append(copy)

    part[...] = jnp.zeros((4, 2, FFN, DIM), F32)

    def widen(block, at, size):
        wide = block.astype(F32)
        for half in range(2):
            e_wide[half, pl.ds(pl.multiple_of(at, 8), size), :] = wide[:, half * 128:(half + 1) * 128]

    for c in range(NESTEP):
        stage_copy(c).wait()

        @pl.loop(0, ESTEP // EBLOCK)
        def _(b):
            at = pl.multiple_of(b * EBLOCK, EBLOCK)
            widen(stage[c % 2, pl.ds(at, EBLOCK), :], c * ESTEP + at, EBLOCK)

        if c + 2 < NESTEP:
            stage_copy(c + 2).start()
    widen(tail_ref[...], NESTEP * ESTEP, ETAIL)

    own_meta.wait()
    for block in (2, 4, 6):
        got_meta(block)
        send_meta(block, 1)
    uid_copies = [pltpu.make_async_copy(meta_out.at[dev(2 * s), 0], uid.at[pl.ds(s * META, META)], uid_sem.at[s]) for s in range(4)]
    for copy in uid_copies:
        copy.start()
    for copy in uid_copies:
        copy.wait()
    own_m.wait()

    def place(i):
        slot = jnp.where(i < PIECES, 0, jnp.where(i < 3 * PIECES, 1 + (i - PIECES) % 2, 3))
        k = jnp.where(i < PIECES, i, jnp.where(i < 3 * PIECES, (i - PIECES) // 2, i - 3 * PIECES))
        return slot, k

    def dx_copies(i, slot, k):
        at = rows_ref.at[pl.ds(pl.multiple_of(dev(2 * slot) * UNIQ + k * PIECE, PIECE), PIECE)]
        return (remote(dx.at[slot, piece(k)], at, dx_send.at[slot, k], dx_recv.at[slot, k], 1),
                pltpu.make_async_copy(dx.at[slot, piece(k)], at, dx_own.at[slot, k]))

    def step(i, carry):
        slot, k = place(i)

        @pl.loop(0, PIECE // 16)
        def _(b):
            base = slot * META + k * PIECE + b * 16
            for j in range(16):
                at = uid[base + j]
                for half in range(2):
                    x_wide[half, pl.ds(b * 16 + j, 1), :] = e_wide[half, pl.ds(at, 1), :]

        here = all_m.at[slot, piece(k)]

        @pl.when(i >= PIECES)
        def _():
            remote(here, here, m_send.at[0, 0], m_recv.at[slot, k], 1).wait_recv()

        @pl.when((slot == 1) & (k % 2 == 0))
        def _():
            remote(here, all_m.at[3, piece(k)], m_send.at[2, k], m_recv.at[3, k], 4).start()

        @pl.when((slot == 2) & (k % 2 == 1))
        def _():
            remote(here, all_m.at[3, piece(k)], m_send.at[2, k], m_recv.at[3, k], 2).start()

        x = jnp.concatenate([x_wide[0], x_wide[1]], axis=1).astype(BF16)
        m = here[...]
        m_hi = m.astype(BF16)
        m_lo = (m - m_hi.astype(F32)).astype(BF16)
        z = dot(x, w1_ref[...], 1, 0).astype(BF16).astype(F32)
        t = jnp.tanh(GELU_C * (z + GELU_A * z * z * z))
        h = (0.5 * z * (1.0 + t)).astype(BF16)
        slope = 0.5 * (1.0 + t) + 0.5 * z * (1.0 - t * t) * GELU_C * (1.0 + 3.0 * GELU_A * z * z)
        dh = (dot(m_hi, w2_ref[...], 1, 1) + dot(m_lo, w2_ref[...], 1, 1)).astype(BF16).astype(F32)
        dz = (dh * slope).astype(BF16)
        dx[slot, piece(k)] = m + dot(dz, w1_ref[...], 1, 1)
        for q in range(FFN // DIM):
            cols = slice(q * DIM, (q + 1) * DIM)
            part[slot, 0, cols] += dot(x, dz[:, cols], 0, 0)
        part[slot, 1] += dot(h, m_hi, 0, 0) + dot(h, m_lo, 0, 0)
        for copy in dx_copies(i, slot, k):
            copy.start()
        return carry

    lax.fori_loop(0, 4 * PIECES, step, 0)

    w_copies = []
    for i in range(2):
        part[0, i] = (part[0, i] + part[1, i]) + (part[2, i] + part[3, i])
        w_copies.append(remote(part.at[0, i], pin.at[i], w_send.at[i], w_recv.at[i], 1))
        w_copies[i].start()
    for i in range(2):
        w_copies[i].wait()
        red_ref[i] = part[0, i] + pin[i]

    @pl.loop(0, 4 * PIECES)
    def _(i):
        slot, k = place(i)
        away, near = dx_copies(i, slot, k)
        away.wait_send()
        near.wait()
        at = rows_ref.at[pl.ds(pl.multiple_of(dev(2 * slot + 1) * UNIQ + k * PIECE, PIECE), PIECE)]
        remote(at, at, dx_send.at[slot, k], dx_recv.at[slot, k], 1).wait_recv()

    for k in range(PIECES):
        here = all_m.at[1 + k % 2, piece(k)]
        remote(here, all_m.at[3, piece(k)], m_send.at[2, k], m_recv.at[3, k], 4 - 2 * (k % 2)).wait_send()
    for block in (1, 3, 5, 7):
        got_meta(block)
    for copy in sent:
        copy.wait_send()


def exchange(m, w1, w2, meta, tail, table):
    vmem = pl.BlockSpec(memory_space=pltpu.VMEM)
    hbm = pl.BlockSpec(memory_space=pl.ANY)
    dma = pltpu.SemaphoreType.DMA
    return pl.pallas_call(
        exchange_kernel,
        out_shape=(jax.ShapeDtypeStruct((NDEV * UNIQ, DIM), F32), jax.ShapeDtypeStruct((NDEV, 1, META), jnp.int32), jax.ShapeDtypeStruct((2, FFN, DIM), F32)),
        in_specs=[hbm, vmem, vmem, vmem, vmem, hbm],
        out_specs=(hbm, vmem, vmem),
        scratch_shapes=[
            pltpu.VMEM((2, NESTEP * ESTEP + ETAIL, 128), F32), pltpu.VMEM((2, ESTEP, DIM), BF16), pltpu.VMEM((4, UNIQ, DIM), F32),
            pltpu.VMEM((2, PIECE, 128), F32), pltpu.VMEM((4, UNIQ, DIM), F32), pltpu.VMEM((4, 2, FFN, DIM), F32), pltpu.VMEM((2, FFN, DIM), F32),
            pltpu.SMEM((4 * META,), jnp.int32),
            dma((2,)), dma((2,)), dma((4,)), dma((3, PIECES)), dma((4, PIECES)), dma((8, 4)), dma((8,)),
            dma((4, PIECES)), dma((4, PIECES)), dma((4, PIECES)), dma((2,)), dma((2,))],
        compiler_params=pltpu.CompilerParams(vmem_limit_bytes=VMEM_LIMIT_MAX, collective_id=0, has_side_effects=True),
        name="exchange",
    )(m, w1, w2, meta, tail, table)


def table_kernel(meta_hbm, rows_hbm, red_hbm, out_hbm, w1_hbm, w2_hbm, *scratch):
    meta = scratch[:NDEV]
    rows, acc, red, meta_sem, in_sem, out_sem, red_sem, w_sem = scratch[NDEV:]

    def in_copy(d, half):
        part = pl.ds(d * UNIQ, UNIQ)
        return pltpu.make_async_copy(rows_hbm.at[part, pl.ds(half * 128, 128)], rows.at[half, part], in_sem.at[d, half])

    def out_copy(c, half):
        part = pl.ds(c * CHUNK, CHUNK if c < NCHUNK - 1 else LAST)
        return pltpu.make_async_copy(acc.at[half, part], out_hbm.at[part, pl.ds(half * 128, 128)], out_sem.at[c, half])

    def meta_copy(d):
        return pltpu.make_async_copy(meta_hbm.at[d, 0], meta[d], meta_sem.at[d])

    for d in range(NDEV):
        meta_copy(d).start()
    for d in range(NDEV):
        for half in range(2):
            in_copy(d, half).start()
    red_in = pltpu.make_async_copy(red_hbm, red, red_sem)
    red_in.start()

    @pl.loop(0, PADDED // ZERO)
    def _(i):
        part = pl.ds(pl.multiple_of(i * ZERO, ZERO), ZERO)
        for half in range(2):
            acc[half, part] = jnp.zeros((ZERO, 128), F32)

    for d in range(NDEV):
        meta_copy(d).wait()
        for half in range(2):
            in_copy(d, half).wait()
    red_in.wait()
    w_out = [pltpu.make_async_copy(red.at[1], w2_hbm, w_sem.at[4])]
    for q in range(FFN // DIM):
        w_out.append(pltpu.make_async_copy(red.at[0, pl.ds(q * DIM, DIM)], w1_hbm.at[:, pl.ds(q * DIM, DIM)], w_sem.at[q]))
    for copy in w_out:
        copy.start()

    for c in range(NCHUNK):
        for d in range(NDEV):
            first = (meta[d][UNIQ + c * CHUNK_HI] + BATCH - 1) // BATCH if c else 0
            last = (meta[d][UNIQ + (c + 1) * CHUNK_HI] + BATCH - 1) // BATCH if c < NCHUNK - 1 else UNIQ // BATCH

            def fetch(b):
                base = pl.multiple_of(b * BATCH, BATCH)
                at = [meta[d][base + k] for k in range(BATCH)]
                sums = []
                for k in range(BATCH):
                    for half in range(2):
                        sums.append(acc[half, pl.ds(at[k], 1), :] + rows[half, pl.ds(d * UNIQ + base + k, 1), :])
                return at, sums

            def put(at, sums):
                for k in range(BATCH):
                    for half in range(2):
                        acc[half, pl.ds(at[k], 1), :] = sums[2 * k + half]

            def step(b, carry):
                ahead = fetch(b)
                put(*carry)
                return ahead

            @pl.when(last > first)
            def _():
                put(*lax.fori_loop(first + 1, last, step, fetch(first)))

        for half in range(2):
            out_copy(c, half).start()
    for copy in w_out:
        copy.wait()
    for c in range(NCHUNK):
        for half in range(2):
            out_copy(c, half).wait()


def table(meta, rows, red):
    hbm = pl.BlockSpec(memory_space=pl.ANY)
    return pl.pallas_call(
        table_kernel,
        in_specs=[hbm] * 3, out_specs=(hbm,) * 3,
        scratch_shapes=[pltpu.SMEM((META,), jnp.int32)] * NDEV + [
            pltpu.VMEM((2, NDEV * UNIQ, 128), F32), pltpu.VMEM((2, PADDED, 128), F32), pltpu.VMEM((2, FFN, DIM), F32),
            pltpu.SemaphoreType.DMA((NDEV,)), pltpu.SemaphoreType.DMA((NDEV, 2)), pltpu.SemaphoreType.DMA((NCHUNK, 2)),
            pltpu.SemaphoreType.DMA, pltpu.SemaphoreType.DMA((5,))],
        out_shape=(jax.ShapeDtypeStruct((VOCAB, DIM), F32), jax.ShapeDtypeStruct((DIM, FFN), F32), jax.ShapeDtypeStruct((FFN, DIM), F32)),
        compiler_params=pltpu.CompilerParams(vmem_limit_bytes=VMEM_LIMIT),
        name="table",
    )(meta, rows, red)


def solution(mesh):
    def per_device(tok_ids, grad_out, n_real, embed_table, w_in, w_out):
        meta, msum = prepare(n_real, tok_ids.reshape(1, TOK), grad_out)
        left = embed_table[NESTEP * ESTEP:].astype(F32)
        left = jnp.pad(left, ((0, ETAIL - left.shape[0]), (0, 0)))
        all_rows, all_meta, red = exchange(msum, w_in, w_out, meta, left, embed_table)
        return table(all_meta, all_rows, red)

    return jax.shard_map(per_device, mesh=mesh, in_specs=(P('data'), P('data', None), P('data'), P(), P(), P()), out_specs=(P(), P(), P()), check_vma=False)
```

time: 119 us -> 95.2 us (0.80)
  local copies, waits for them, and re-layouts: 12.9 us -> 0.76 us
  Pallas kernels: 104 us -> 92.1 us
    pallas_call x1, Pallas kernels: 69.2 us -> 55.8 us  [exchange(): pl.pallas_call(exchange_kernel, out_shape=(jax.ShapeDtypeStruct((NDEV * U...]
    gather x1 -> x0, local copies, waits for them, and re-layouts: 12.2 us -> none  [per_device(): x = jnp.take(embed_table, meta[0, :UNIQ], axis=0, mode='clip')]
where the time goes in v7:
time: 95.2 us; the launch traced here: 94.8 us
  Pallas kernels  92.1 us (97%)
  between operations  1.29 us (1%)
    pallas_call x1, Pallas kernels, exchange(): pl.pallas_call(exchange_kernel, out_shape=(jax.ShapeDtypeStruct((NDEV * U...  55.8 us
    pallas_call x1, Pallas kernels, table(): pl.pallas_call(table_kernel, in_specs=[hbm] * 3, out_specs=(hbm,) * 3, sc...  25.8 us
    pallas_call x1, Pallas kernels, prepare(): pl.pallas_call(prepare_kernel, out_shape=(jax.ShapeDtypeStruct((1, META),...  10.5 us

profile of v7, /device:TPU:0, one launch (start us, length us, event | category | flops | bytes accessed | tf_op | source)
XLA Modules:
  0.0 94.8 jit_solution(10460890686210732628)
XLA Ops:
  1.3 0.8 slice.3
  2.0 0.6 pad_convert_fusion.tail_ref
  2.7 10.5 %prepare.1 = (s32[1,1152]{1,0:T(1,128)}, f32[1024,256]{1,0:T(8,128)}) custom-call(s32[1]{0:T(128)S(6)} %copy.9.n_ref, s32[1,4096]{1,0:T(1,128)} %bitcast.1, bf16[4096,256]{1,0:T(8,128)(2,1)} %dy_ref.1), custom_call_target="tpu_custom_call" | custom-call | tf_op jit(solution)/shard_map/prepare/pallas_call | solution.py:99
  13.2 55.8 %exchange.1 = (f32[8192,256]{1,0:T(8,128)}, s32[8,1,1152]{2,1,0:T(1,128)}, f32[2,1024,256]{2,1,0:T(8,128)}) custom-call(f32[1024,256]{1,0:T(8,128)} %get-tuple-element.8.m_hbm, bf16[256,1024]{1,0:T(8,128)(2,1)} %w1_ref.1, bf16[1024,256]{1,0:T(8,128)(2,1)} %w2_ref.1, s32[1,1152]{1,0:T(1,128)} %get-tuple-element.9.meta_ref, ...), custom_call_target="tpu_custom_call" | custom-call | tf_op jit(solution)/shard_map/exchange/pallas_call | solution.py:276
  69.0 25.8 %table.1 = (f32[30522,256]{1,0:T(8,128)}, f32[256,1024]{1,0:T(8,128)}, f32[1024,256]{1,0:T(8,128)}) custom-call(s32[8,1,1152]{2,1,0:T(1,128)} %get-tuple-element.10.meta_hbm, f32[8192,256]{1,0:T(8,128)} %get-tuple-element.11.rows_hbm, f32[2,1024,256]{2,1,0:T(8,128)} %get-tuple-element.12.red_hbm), custom_call_target="tpu_custom_call" | custom-call | tf_op jit(solution)/shard_map/table/pallas_call | solution.py:371
